TPU v7x, 32 devices: a whole 2x2x4 slice. The times are simulated.
32 devices in a mesh: seq: 8 (over z, core), fsdp: 4 (over y, x).
Axes of the slice: x: 2, y: 2, z: 4, core: 2. Of those that a mesh axis runs over, the one named last changes fastest.
Arguments:
- tokens: bfloat16 [4, 1024, 2048], P('fsdp', 'seq'), may hold values from -6 to 6
- ln_gain: bfloat16 [2048], P('fsdp'), may hold values from 0.5 to 1.5
- ln_bias: bfloat16 [2048], P('fsdp'), may hold values from -3 to 3
- qkv_weight: bfloat16 [2048, 6144], P('fsdp')
- qkv_bias: bfloat16 [6144], P('fsdp'), may hold values from -3 to 3
- dense_weight: bfloat16 [2048, 2048], P('fsdp'), may hold values from -0.5 to 0.5
- dense_bias: bfloat16 [2048], P('fsdp'), may hold values from -3 to 3
- fc1_weight: bfloat16 [2048, 8192], P('fsdp'), may hold values from -0.125 to 0.125
- fc1_bias: bfloat16 [8192], P('fsdp'), may hold values from -3 to 3
- fc2_weight: bfloat16 [8192, 2048], P('fsdp'), may hold values from -0.0625 to 0.0625
- fc2_bias: bfloat16 [2048], P('fsdp'), may hold values from -3 to 3
- segments: int32 [4, 1024], P('fsdp'), may hold values from 0 to 1, as said below
- positions: int32 [4, 1024], P('fsdp', 'seq'), may hold values from 0 to 2046, as said below
- cotangent: bfloat16 [4, 1024, 2048], P('fsdp', 'seq'), may hold values from -6 to 6
Outputs:
- out: bfloat16 [4, 1024, 2048], P('fsdp', 'seq')
- grad_tokens: float32 [4, 1024, 2048], P('fsdp', 'seq')
- grad_ln_gain: float32 [2048], P('fsdp')
- grad_ln_bias: float32 [2048], P('fsdp')
- grad_qkv_weight: float32 [2048, 6144], P('fsdp')
- grad_qkv_bias: float32 [6144], P('fsdp')
- grad_dense_weight: float32 [2048, 2048], P('fsdp')
- grad_dense_bias: float32 [2048], P('fsdp')
- grad_fc1_weight: float32 [2048, 8192], P('fsdp')
- grad_fc1_bias: float32 [8192], P('fsdp')
- grad_fc2_weight: float32 [8192, 2048], P('fsdp')
- grad_fc2_bias: float32 [2048], P('fsdp')
Inputs may be any that keep to these rules, and one draw needn't show every extreme that they name: `segments`: document numbers never fall along a sequence and each of 0 to 1 occurs in every sequence. The first document of each sequence starts at position 0; positions rise by one from token to token within a document; in every sequence the last token of the last document has position 2046.
All inputs are finite; a program needn't handle non-finite values.
Results may differ from a plain program's by a relative error of at most 0.0095.
Values may be sent and summed in bfloat16 or wider, within the bound.
A program may use at most 448 MiB of HBM per device.

v0:
```python
import jax
import jax.numpy as jnp
from jax import lax
from jax.sharding import PartitionSpec as P

HEADS = 32
HEAD = 64
ROT = 32


norm_epsilon = 1e-05


def rotary_angles(pos_row, rot_width):
    inverse = 1.0 / 10000.0 ** (jnp.arange(0, rot_width, 2, dtype=jnp.float32) / rot_width)
    return pos_row.astype(jnp.float32)[:, None] * inverse[None, :]


def rotate_pair(values_in, angles):
    half_width = angles.shape[-1]
    cosine = jnp.cos(angles)[:, None, None, :]
    sine_part = jnp.sin(angles)[:, None, None, :]
    low_half = values_in[..., :half_width]
    high_half = values_in[..., half_width : 2 * half_width]
    rest_part = values_in[..., 2 * half_width :]
    return jnp.concatenate(
        [
            low_half * cosine - high_half * sine_part,
            high_half * cosine + low_half * sine_part,
            rest_part,
        ],
        axis=-1,
    )


def gelu_tanh(values_in):
    return jax.nn.gelu(values_in, approximate=True)


def contract_rows(left_side, right_side):
    return lax.dot_general(
        left_side, right_side, (((0,), (0,)), ((), ())), preferred_element_type=jnp.float32
    )


def contract_cols(left_side, right_side):
    return lax.dot_general(
        left_side, right_side, (((1,), (1,)), ((), ())), preferred_element_type=jnp.float32
    )


def block_scores(query_block, keys_all, first_row, seg_row):
    block_len = query_block.shape[0]
    seq_len = keys_all.shape[0]
    score_scale = query_block.shape[2] ** (-0.5)
    scores = (
        jnp.einsum("qhd,khd->hqk", query_block, keys_all, preferred_element_type=jnp.float32)
        * score_scale
    )
    query_place = first_row + jnp.arange(block_len)
    key_place = jnp.arange(seq_len)
    query_seg = lax.dynamic_slice_in_dim(seg_row, first_row, block_len, 0)
    allowed = (key_place[None, :] <= query_place[:, None]) & (
        query_seg[:, None] == seg_row[None, :]
    )
    return (jnp.where(allowed[None], scores, -1e30), allowed)


def attend_forward(queries, keys_all, values, seg_row):
    seq_len = queries.shape[0]
    block_len = min(512, seq_len)
    count_blocks = seq_len // block_len

    def one_block(block_index):
        first_row = block_index * block_len
        query_block = lax.dynamic_slice_in_dim(queries, first_row, block_len, 0)
        scores, allowed = block_scores(query_block, keys_all, first_row, seg_row)
        row_top = jnp.max(scores, axis=-1, keepdims=True)
        raised = jnp.exp(scores - row_top)
        row_total = jnp.sum(raised, axis=-1, keepdims=True)
        probabilities = raised / row_total
        result = jnp.einsum(
            "hqk,khd->qhd",
            probabilities.astype(jnp.bfloat16),
            values,
            preferred_element_type=jnp.float32,
        )
        return (result, row_top[..., 0] + jnp.log(row_total[..., 0]))

    outputs, log_norm = lax.map(one_block, jnp.arange(count_blocks))
    return (outputs.reshape(seq_len, queries.shape[1], queries.shape[2]), log_norm)


def attend_backward(queries, keys_all, values, seg_row, log_norm, grad_out):
    seq_len = queries.shape[0]
    block_len = min(512, seq_len)
    count_blocks = seq_len // block_len
    score_scale = queries.shape[2] ** (-0.5)

    def one_block(running, block_index):
        grad_keys, grad_values = running
        first_row = block_index * block_len
        query_block = lax.dynamic_slice_in_dim(queries, first_row, block_len, 0)
        grad_block = lax.dynamic_slice_in_dim(grad_out, first_row, block_len, 0)
        scores, allowed = block_scores(query_block, keys_all, first_row, seg_row)
        probabilities = jnp.where(
            allowed[None], jnp.exp(scores - log_norm[block_index][..., None]), 0.0
        )
        grad_probs = jnp.einsum(
            "qhd,khd->hqk", grad_block, values, preferred_element_type=jnp.float32
        )
        row_inner = jnp.sum(probabilities * grad_probs, axis=-1, keepdims=True)
        grad_scores = (probabilities * (grad_probs - row_inner)).astype(jnp.bfloat16)
        grad_query = (
            jnp.einsum("hqk,khd->qhd", grad_scores, keys_all, preferred_element_type=jnp.float32)
            * score_scale
        )
        grad_keys = (
            grad_keys
            + jnp.einsum(
                "hqk,qhd->khd", grad_scores, query_block, preferred_element_type=jnp.float32
            )
            * score_scale
        )
        grad_values = grad_values + jnp.einsum(
            "hqk,qhd->khd",
            probabilities.astype(jnp.bfloat16),
            grad_block,
            preferred_element_type=jnp.float32,
        )
        return ((grad_keys, grad_values), grad_query)

    zeros_start = jnp.zeros(keys_all.shape, jnp.float32)
    (grad_keys, grad_values), grad_queries = lax.scan(
        one_block, (zeros_start, zeros_start), jnp.arange(count_blocks)
    )
    return (grad_queries.reshape(queries.shape), grad_keys, grad_values)


def body(
    tokens,
    ln_gain,
    ln_bias,
    qkv_weight,
    qkv_bias,
    dense_weight,
    dense_bias,
    fc1_weight,
    fc1_bias,
    fc2_weight,
    fc2_bias,
    segments,
    positions,
    cotangent,
):
    seq_count = lax.axis_size("seq")
    shard_count = lax.axis_size("fsdp")
    gathered = (
        lax.all_gather(qkv_weight, "fsdp", axis=0, tiled=True),
        lax.all_gather(dense_weight, "fsdp", axis=0, tiled=True),
        lax.all_gather(fc1_weight, "fsdp", axis=0, tiled=True),
        lax.all_gather(fc2_weight, "fsdp", axis=0, tiled=True),
        lax.all_gather(ln_gain, "fsdp", axis=0, tiled=True),
        lax.all_gather(ln_bias, "fsdp", axis=0, tiled=True),
        lax.all_gather(qkv_bias, "fsdp", axis=0, tiled=True),
        lax.all_gather(dense_bias, "fsdp", axis=0, tiled=True),
        lax.all_gather(fc1_bias, "fsdp", axis=0, tiled=True),
        lax.all_gather(fc2_bias, "fsdp", axis=0, tiled=True),
    )
    w_qkv, w_dense, w_up, w_down = (gathered[0], gathered[1], gathered[2], gathered[3])
    gain_full, shift_full, b_qkv, b_dense, b_up, b_down = (
        gathered[4],
        gathered[5],
        gathered[6],
        gathered[7],
        gathered[8],
        gathered[9],
    )
    tok_len = tokens.shape[1]
    model_width = tokens.shape[2]
    heads_here = HEADS // seq_count
    head_slab = heads_here * HEAD
    inputs = tokens[0].astype(jnp.float32)
    centre = jnp.mean(inputs, axis=-1, keepdims=True)
    variance = jnp.mean((inputs - centre) ** 2, axis=-1, keepdims=True)
    inv_std = lax.rsqrt(variance + norm_epsilon)
    standard = (inputs - centre) * inv_std
    normed = (standard * gain_full.astype(jnp.float32) + shift_full.astype(jnp.float32)).astype(
        jnp.bfloat16
    )
    projected = jnp.dot(normed, w_qkv, preferred_element_type=jnp.float32) + b_qkv.astype(
        jnp.float32
    )
    projected = projected.reshape(tok_len, 3, HEADS, HEAD)
    angles = rotary_angles(positions[0], ROT)
    turned = jnp.concatenate(
        [rotate_pair(projected[:, :2], angles), projected[:, 2:]], axis=1
    ).astype(jnp.bfloat16)
    outgoing = turned.reshape(tok_len, 3, seq_count, head_slab)
    by_heads = lax.all_to_all(outgoing, "seq", split_axis=2, concat_axis=0, tiled=True)
    seq_len = by_heads.shape[0]
    by_heads = by_heads.reshape(seq_len, 3, heads_here, HEAD)
    queries, keys_all, values = (by_heads[:, 0], by_heads[:, 1], by_heads[:, 2])
    seg_row = segments[0]
    attended, log_norm = attend_forward(queries, keys_all, values, seg_row)
    returned_heads = lax.all_to_all(
        attended.astype(jnp.bfloat16).reshape(seq_len, 1, head_slab),
        "seq",
        split_axis=0,
        concat_axis=1,
        tiled=True,
    )
    att_tokens = returned_heads.reshape(tok_len, model_width)
    branch_att = jnp.dot(att_tokens, w_dense, preferred_element_type=jnp.float32) + b_dense.astype(
        jnp.float32
    )
    pre_act = jnp.dot(normed, w_up, preferred_element_type=jnp.float32) + b_up.astype(jnp.float32)
    activated = gelu_tanh(pre_act).astype(jnp.bfloat16)
    branch_mlp = jnp.dot(activated, w_down, preferred_element_type=jnp.float32) + b_down.astype(
        jnp.float32
    )
    result = (inputs + branch_att + branch_mlp).astype(jnp.bfloat16)
    regathered = (
        lax.all_gather(qkv_weight, "fsdp", axis=0, tiled=True),
        lax.all_gather(dense_weight, "fsdp", axis=0, tiled=True),
        lax.all_gather(fc1_weight, "fsdp", axis=0, tiled=True),
        lax.all_gather(fc2_weight, "fsdp", axis=0, tiled=True),
        lax.all_gather(ln_gain, "fsdp", axis=0, tiled=True),
        lax.all_gather(ln_bias, "fsdp", axis=0, tiled=True),
        lax.all_gather(qkv_bias, "fsdp", axis=0, tiled=True),
        lax.all_gather(dense_bias, "fsdp", axis=0, tiled=True),
        lax.all_gather(fc1_bias, "fsdp", axis=0, tiled=True),
        lax.all_gather(fc2_bias, "fsdp", axis=0, tiled=True),
    )
    w_qkv, w_dense, w_up, w_down = (regathered[0], regathered[1], regathered[2], regathered[3])
    gain_full = regathered[4]
    upstream = cotangent[0]
    grad_act = contract_cols(upstream, w_down)
    grad_slope = jax.vjp(gelu_tanh, pre_act)[1](grad_act)[0]
    grad_pre = grad_slope.astype(jnp.bfloat16)
    grad_att = contract_cols(upstream, w_dense).astype(jnp.bfloat16)
    heads_grad = lax.all_to_all(
        grad_att.reshape(tok_len, seq_count, head_slab),
        "seq",
        split_axis=1,
        concat_axis=0,
        tiled=True,
    )
    heads_grad = heads_grad.reshape(seq_len, heads_here, HEAD)
    grad_q, grad_k, grad_v = attend_backward(
        queries, keys_all, values, seg_row, log_norm, heads_grad
    )
    stacked = (
        jnp.stack([grad_q, grad_k, grad_v], axis=1)
        .astype(jnp.bfloat16)
        .reshape(seq_len, 3, 1, head_slab)
    )
    returned = lax.all_to_all(stacked, "seq", split_axis=0, concat_axis=2, tiled=True)
    returned = returned.reshape(tok_len, 3, HEADS, HEAD).astype(jnp.float32)
    unturned = jnp.concatenate([rotate_pair(returned[:, :2], -angles), returned[:, 2:]], axis=1)
    grad_mixed = unturned.reshape(tok_len, 3 * model_width).astype(jnp.bfloat16)
    grad_normed = contract_cols(grad_mixed, w_qkv) + contract_cols(grad_pre, w_up)
    scaled = grad_normed * gain_full.astype(jnp.float32)
    grad_inputs = upstream.astype(jnp.float32) + inv_std * (
        scaled
        - jnp.mean(scaled, axis=-1, keepdims=True)
        - standard * jnp.mean(scaled * standard, axis=-1, keepdims=True)
    )
    gain_term = jnp.sum(grad_normed * standard, axis=0)
    shift_term = jnp.sum(grad_normed, axis=0)
    qkv_term = jnp.sum(grad_mixed.astype(jnp.float32), axis=0)
    out_term = jnp.sum(upstream.astype(jnp.float32), axis=0)
    up_term = jnp.sum(grad_pre.astype(jnp.float32), axis=0)

    def spread_vec(vector):
        return vector.reshape(shard_count, seq_count, -1).transpose(1, 0, 2).reshape(-1)

    vector_parts = (
        lax.psum_scatter(spread_vec(gain_term), ("seq", "fsdp"), scatter_dimension=0, tiled=True),
        lax.psum_scatter(spread_vec(shift_term), ("seq", "fsdp"), scatter_dimension=0, tiled=True),
        lax.psum_scatter(spread_vec(qkv_term), ("seq", "fsdp"), scatter_dimension=0, tiled=True),
        lax.psum_scatter(spread_vec(out_term), ("seq", "fsdp"), scatter_dimension=0, tiled=True),
        lax.psum_scatter(spread_vec(up_term), ("seq", "fsdp"), scatter_dimension=0, tiled=True),
    )
    ff_width = w_up.shape[1]
    col_qkv = 3 * model_width // seq_count
    col_up = ff_width // seq_count
    row_dense = model_width // (shard_count * seq_count)
    row_down = ff_width // (shard_count * seq_count)
    normed_full, upstream_full = (
        lax.all_gather(normed, "seq", axis=0, tiled=True),
        lax.all_gather(upstream, "seq", axis=0, tiled=True),
    )
    grads_cols = (
        lax.all_to_all(
            grad_mixed.reshape(tok_len, seq_count, col_qkv),
            "seq",
            split_axis=1,
            concat_axis=0,
            tiled=True,
        ),
        lax.all_to_all(
            grad_pre.reshape(tok_len, seq_count, col_up),
            "seq",
            split_axis=1,
            concat_axis=0,
            tiled=True,
        ),
    )
    mixed_cols = grads_cols[0].reshape(seq_len, col_qkv)
    pre_cols = grads_cols[1].reshape(seq_len, col_up)
    rows_sel = (
        lax.all_to_all(
            att_tokens.reshape(tok_len, shard_count, seq_count, row_dense),
            "seq",
            split_axis=2,
            concat_axis=0,
            tiled=True,
        ),
        lax.all_to_all(
            activated.reshape(tok_len, shard_count, seq_count, row_down),
            "seq",
            split_axis=2,
            concat_axis=0,
            tiled=True,
        ),
    )
    att_sel = rows_sel[0].reshape(seq_len, shard_count * row_dense)
    down_sel = rows_sel[1].reshape(seq_len, shard_count * row_down)

    def moved_sum(left_full, right_side):
        return lax.psum_scatter(
            contract_rows(left_full, right_side).astype(jnp.bfloat16),
            "fsdp",
            scatter_dimension=0,
            tiled=True,
        ).astype(jnp.float32)

    piece_qkv = moved_sum(normed_full, mixed_cols)
    piece_dense = moved_sum(att_sel, upstream_full)
    piece_up = moved_sum(normed_full, pre_cols)
    piece_down = moved_sum(down_sel, upstream_full)
    reduced = (
        lax.all_gather(piece_qkv.astype(jnp.bfloat16), "seq", axis=1, tiled=True).astype(
            piece_qkv.dtype
        ),
        lax.all_gather(piece_dense.astype(jnp.bfloat16), "seq", axis=0, tiled=True).astype(
            piece_dense.dtype
        ),
        lax.all_gather(piece_up.astype(jnp.bfloat16), "seq", axis=1, tiled=True).astype(
            piece_up.dtype
        ),
        lax.all_gather(piece_down.astype(jnp.bfloat16), "seq", axis=0, tiled=True).astype(
            piece_down.dtype
        ),
        lax.all_gather(vector_parts[0].astype(jnp.bfloat16), "seq", axis=0, tiled=True).astype(
            jnp.float32
        ),
        lax.all_gather(vector_parts[1].astype(jnp.bfloat16), "seq", axis=0, tiled=True).astype(
            jnp.float32
        ),
        lax.all_gather(vector_parts[2].astype(jnp.bfloat16), "seq", axis=0, tiled=True).astype(
            jnp.float32
        ),
        lax.all_gather(vector_parts[3].astype(jnp.bfloat16), "seq", axis=0, tiled=True).astype(
            jnp.float32
        ),
        lax.all_gather(vector_parts[4].astype(jnp.bfloat16), "seq", axis=0, tiled=True).astype(
            jnp.float32
        ),
    )
    return (
        result[None],
        grad_inputs[None],
        reduced[4],
        reduced[5],
        reduced[0],
        reduced[6],
        reduced[1],
        reduced[7],
        reduced[2],
        reduced[8],
        reduced[3],
        reduced[7],
    )


def solution(mesh):
    return jax.shard_map(
        body,
        mesh=mesh,
        in_specs=(
            P("fsdp", "seq", None),
            P("fsdp"),
            P("fsdp"),
            P("fsdp", None),
            P("fsdp"),
            P("fsdp", None),
            P("fsdp"),
            P("fsdp", None),
            P("fsdp"),
            P("fsdp", None),
            P("fsdp"),
            P("fsdp", None),
            P("fsdp", "seq"),
            P("fsdp", "seq", None),
        ),
        out_specs=(
            P("fsdp", "seq", None),
            P("fsdp", "seq", None),
            P("fsdp"),
            P("fsdp"),
            P("fsdp", None),
            P("fsdp"),
            P("fsdp", None),
            P("fsdp"),
            P("fsdp", None),
            P("fsdp"),
            P("fsdp", None),
            P("fsdp"),
        ),
        check_vma=False,
    )
```

profile of v0, /device:TPU:0, one launch (start us, length us, event | category | flops | bytes accessed | tf_op | source)
XLA Modules:
  0.0 1528.9 jit_solution(6657508894019280868)
XLA Ops:
  9.5 9.6 all-gather.1
  19.1 8.2 all-gather.2
  30.9 7.7 all-gather.3
  39.4 60.9 %all-gather.20.cloned.1.call-done = bf16[2048,2048]{1,0:T(8,128)(2,1)} async-done(((bf16[512,2048]{1,0:T(8,128)(2,1)}), bf16[2048,2048]{1,0:T(8,128)(2,1)}) %all-gather.20.cloned.1.call-update) | async-done | bytes 8388624 | tf_op jit(solution)/shard_map/all_gather | solution.py:160
  112.0 217.8 %all-gather.18.cloned.1.call-done = bf16[2048,6144]{1,0:T(8,128)(2,1)} async-done(((bf16[512,6144]{1,0:T(8,128)(2,1)}), bf16[2048,6144]{1,0:T(8,128)(2,1)}) %all-gather.18.cloned.1.call-update) | async-done | bytes 25165840 | tf_op jit(solution)/shard_map/all_gather | solution.py:159
  329.8 13.3 convolution_add_fusion.1
  354.1 56.5 %all-to-all-done = bf16[128,3,8,256]{0,3,1,2:T(8,128)(2,1)} async-done(((bf16[128,3,8,256]{0,3,1,2:T(8,128)(2,1)}), bf16[128,3,8,256]{0,3,1,2:T(8,128)(2,1)}, u32[]{:S(2)}, u32[]{:S(2)}) %all-to-all-start) | async-done | bytes 1572896 | tf_op jit(solution)/shard_map/all_to_all | solution.py:200
  421.2 20.8 %while.27 = (s32[]{:T(128)}, bf16[2,512,4,64]{1,3,2,0:T(8,128)(2,1)}, f32[2,4,512]{2,1,0:T(4,128)S(1)}, s32[2]{0:T(128)S(1)}, s32[1024]{0:T(1024)S(1)}, /*index=...) while((s32[]{:T(128)}, ...), condition=%wide.region_5.6_spmd, body=%wide.region_2.5_spmd.sunk | while | flops 563608064 | bytes 31275748 | solution.py:90
  462.7 61.2 %while.28 = (s32[]{:T(128)}, f32[1024,4,64]{0,2,1:T(8,128)S(1)}, f32[1024,4,64]{0,2,1:T(8,128)S(1)}, bf16[2,512,4,64]{1,3,2,0:T(8,128)(2,1)}, s32[2]{0:T(128)S(1...) while((s32[]{:T(128)}, f32[1024,4,64]{0,2,1:T(8,128)S(1)}, ...), condition=%wide.region_8.9_spmd.clone, body=%wide.region_6.8_spmd.clone.sunk | while | flops 1366161920 | bytes 180411312 | solution.py:134
  474.0 7.5 multiply_reduce_fusion.3
  539.1 43.7 %all-to-all-done.3 = bf16[1024,3,1,256]{3,1,2,0:T(4,128)(2,1)S(1)} async-done(((bf16[1024,3,1,256]{3,1,2,0:T(4,128)(2,1)}), bf16[1024,3,1,256]{3,1,2,0:T(4,128)(2,1)S(1)}, u32[]{:S(2)}, u32[]{:S(2)}) %all-to-all-start.3) | async-done | bytes 1572896 | tf_op jit(solution)/shard_map/all_to_all | solution.py:258
  612.0 8.7 all_gather.75
  620.7 22.9 %all-to-all-done.4 = bf16[128,8,768]{0,2,1:T(8,128)(2,1)S(1)} async-done(((bf16[128,8,768]{0,2,1:T(8,128)(2,1)}), bf16[128,8,768]{0,2,1:T(8,128)(2,1)S(1)}, u32[]{:S(2)}, u32[]{:S(2)}) %all-to-all-start.4) | async-done | bytes 1572896 | tf_op jit(solution)/shard_map/all_to_all | solution.py:295
  651.9 99.4 %all-gather.22.cloned.1.call-done = bf16[2048,8192]{1,0:T(8,128)(2,1)} async-done(((bf16[512,8192]{1,0:T(8,128)(2,1)}), bf16[2048,8192]{1,0:T(8,128)(2,1)}) %all-gather.22.cloned.1.call-update) | async-done | bytes 33554448 | tf_op jit(solution)/shard_map/all_gather | solution.py:161
  751.3 19.0 %multiply_convert_fusion.1 = (bf16[128,8192]{1,0:T(8,128)(2,1)}, f32[128,8192]{1,0:T(8,128)}) fusion(f32[8192]{0:T(1024)S(1)} %convert_element_type.189, bf16[128,2048]{1,0:T(8,128)(2,1)S(1)} %copy-done.10, bf16[2048,8192]{1,0:T(8,128)(2,1)} %all-gather.22.cloned.1.call-done), kind=kOutput, calls=%fused_computation.59 | convolution fusion | flops 4305453056 | bytes 40402944 | tf_op jit(solution)/shard_map/dot_general | solution.py:217
  770.3 279.8 %all-gather.24.cloned.1.call-done = bf16[8192,2048]{1,0:T(8,128)(2,1)} async-done(((bf16[2048,2048]{1,0:T(8,128)(2,1)}), bf16[8192,2048]{1,0:T(8,128)(2,1)}) %all-gather.24.cloned.1.call-update) | async-done | bytes 33554448 | tf_op jit(solution)/shard_map/all_gather | solution.py:162
  1050.1 18.0 %convert_reduce_fusion = (f32[8192]{0:T(1024)S(1)}, bf16[128,8192]{1,0:T(8,128)(2,1)S(1)}) fusion(f32[128,8192]{1,0:T(8,128)} %get-tuple-element.255, bf16[8192,2048]{1,0:T(8,128)(2,1)} %all-gather.24.cloned.1.call-done, bf16[1,128,2048]{2,1,0:T(8,128)(2,1)S(1)} %copy-done.12), kind=kOutput, calls=%fused_computation.58 | convolution fusion | flops 4318027776 | bytes 40402944 | tf_op jit(solution)/shard_map/dot_general | solution.py:47
  1068.3 53.7 %all_to_all.114 = bf16[128,8,1024]{2,0,1:T(8,128)(2,1)S(1)} all-to-all(bf16[128,8,1024]{2,0,1:T(8,128)(2,1)S(1)} %bitcast.256), channel_id=1, replica_groups=mesh['seq'=8,'fsdp'=4] {'seq'}, dimensions={1} | all-to-all | bytes 4194304 | tf_op jit(solution)/shard_map/all_to_all | solution.py:302
  1136.4 53.1 %all_to_all.115 = bf16[128,4,8,256]{0,3,1,2:T(8,128)(2,1)S(1)} all-to-all(bf16[128,4,8,256]{0,3,1,2:T(8,128)(2,1)} %copy.127), channel_id=1, replica_groups=mesh['seq'=8,'fsdp'=4] {'seq'}, dimensions={2} | all-to-all | bytes 4194304 | tf_op jit(solution)/shard_map/all_to_all | solution.py:320
  1199.1 48.6 %reduce-scatter.11.cloned.1.call-done = bf16[256,2048]{1,0:T(8,128)(2,1)} async-done(((bf16[1024,2048]{1,0:T(8,128)(2,1)}), bf16[256,2048]{1,0:T(8,128)(2,1)}) %reduce-scatter.11.cloned.1.call-update) | async-done | bytes 1048592 | tf_op jit(solution)/shard_map/reduce_scatter | solution.py:332
  1249.6 8.0 all-gather.4
  1270.8 14.3 fusion.80
  1289.5 17.7 %fusion.68 = (f32[2048]{0:T(1024)S(1)}, f32[128]{0:T(128)S(1)}, f32[128]{0:T(128)S(1)}, f32[2048]{0:T(1024)S(1)}, f32[128,2048]{1,0:T(8,128)}) fusion(bf16[1,128,2048]{2,1,0:T(8,128)(2,1)S(1)} %copy-done.4, f32[128]{0:T(128)S(1)} %copy-done.23, f32[128]{0:T(128)S(1)} %copy-done.21, f32[2048]{0:T(1024)S(1)} %bitcast.281, f32[128,2048]{1,0:T(8,128)} %fusion.80, ...), kind=kOutput, calls=%fused_computation.96 | convolution fusion | flops 4297846784 | bytes 38299648 | tf_op jit(solution)/shard_map/dot_general | solution.py:47
  1310.6 43.6 %all-reduce.9 = (bf16[2048]{0:T(1024)(128)(2,1)S(1)}, bf16[2048]{0:T(1024)(128)(2,1)S(1)}, bf16[6144]{0:T(1024)(128)(2,1)S(1)}, bf16[2048]{0:T(1024)(128)(2,1)S(1)}, bf16[8192]{0:T(1024)(128)(2,1)S(1)}) all-reduce(f32[2048]{0:T(1024)S(1)} %reshape.440, ...), channel_id=3, replica_groups=mesh['seq'=8,'fsdp'=4] {'seq','fsdp'}, use_global_device_ids=true, to_apply=%region_12.13.clone | all-reduce | flops 20480 | bytes 122880
  1355.5 15.7 %all-reduce.10 = (bf16[512]{0:T(512)(128)(2,1)S(1)}, bf16[512]{0:T(512)(128)(2,1)S(1)}, bf16[1536]{0:T(1024)(128)(2,1)S(1)}, bf16[512]{0:T(512)(128)(2,1)S(1)}) all-reduce(bf16[512]{0:T(512)(128)(2,1)S(1)} %dynamic-update-slice, bf16[512]{0:T(512)(128)(2,1)S(1)} %dynamic-update-slice.1, ...), channel_id=1, replica_groups=mesh['seq'=8,'fsdp'=4] {'seq'}, use_global_device_ids=true, to_apply=%add | all-reduce | flops 3072 | bytes 12288
  1373.0 11.5 all-gather.6
  1385.2 14.4 fusion.53
  1399.6 9.3 convert_element_type.208
  1408.9 19.1 %all-gather.32.cloned.1.call-done = bf16[512,8192]{1,0:T(8,128)(2,1)} async-done(((bf16[512,1024]{1,0:T(8,128)(2,1)}), bf16[512,8192]{1,0:T(8,128)(2,1)}) %all-gather.32.cloned.1.call-update) | async-done | bytes 8388624 | tf_op jit(solution)/shard_map/all_gather | solution.py:350
  1428.0 12.5 convert_element_type.217
  1440.5 69.5 %all-gather.34.cloned.1.call-done = bf16[2048,2048]{1,0:T(8,128)(2,1)} async-done(((bf16[256,2048]{1,0:T(8,128)(2,1)}), bf16[2048,2048]{1,0:T(8,128)(2,1)}) %all-gather.34.cloned.1.call-update) | async-done | bytes 8388624 | tf_op jit(solution)/shard_map/all_gather | solution.py:353
  1510.0 11.7 convert_element_type.222
  (281 shorter events, 230.4 us)
Async XLA Ops:
  7.2 93.1 %all-gather.20.cloned.1.call-start = ((), (), s32[]{:S(2)}) async-start(), calls=%async_computation.13 | async-start | bytes 10485760 | tf_op jit(solution)/shard_map/all_gather | solution.py:160
  7.9 321.8 %all-gather.18.cloned.1.call-start = ((), (), s32[]{:S(2)}) async-start(), calls=%async_computation.12 | async-start | bytes 31457280 | tf_op jit(solution)/shard_map/all_gather | solution.py:159
  8.7 598.8 %all-gather.36.cloned.1.call-start = ((), (), s32[]{:S(2)}) async-start(), calls=%async_computation.25 | async-start | bytes 4718592 | tf_op jit(solution)/shard_map/all_gather | solution.py:292
  9.4 634.9 %all-gather.26.cloned.1.call-start = ((), (), s32[]{:S(2)}) async-start(), calls=%async_computation.16 | async-start | bytes 4718592 | tf_op jit(solution)/shard_map/all_gather | solution.py:291
  29.6 721.7 %all-gather.22.cloned.1.call-start = ((), (), s32[]{:S(2)}) async-start(), calls=%async_computation.14 | async-start | bytes 41943040 | tf_op jit(solution)/shard_map/all_gather | solution.py:161
  30.2 70.1 %copy-start.11 = (bf16[1,128,2048]{2,1,0:T(8,128)(2,1)S(1)}, bf16[1,128,2048]{2,1,0:T(8,128)(2,1)}, u32[]{:S(2)}) copy-start(bf16[1,128,2048]{2,1,0:T(8,128)(2,1)} %param.31) | copy-start | bytes 1572868
  30.2 1019.9 %all-gather.24.cloned.1.call-start = ((), (), s32[]{:S(2)}) async-start(), calls=%async_computation.15 | async-start | bytes 41943040 | tf_op jit(solution)/shard_map/all_gather | solution.py:162
  39.4 290.4 %copy-start.9 = (bf16[128,2048]{1,0:T(8,128)(2,1)S(1)}, bf16[128,2048]{1,0:T(8,128)(2,1)}, u32[]{:S(2)}) copy-start(bf16[128,2048]{1,0:T(8,128)(2,1)} %fusion.64) | copy-start | bytes 1572868
  107.4 240.2 %all-to-all-start.2 = ((bf16[128,8,256]{2,0,1:T(8,128)(2,1)}), bf16[128,8,256]{2,0,1:T(8,128)(2,1)}, u32[]{:S(2)}, u32[]{:S(2)}) async-start(bf16[128,8,256]{2,0,1:T(8,128)(2,1)} %bitcast.210), calls=%async_computation.2 | async-start | bytes 1048576 | tf_op jit(solution)/shard_map/all_to_all | solution.py:242
  347.6 63.0 %all-to-all-start = ((bf16[128,3,8,256]{0,3,1,2:T(8,128)(2,1)}), bf16[128,3,8,256]{0,3,1,2:T(8,128)(2,1)}, u32[]{:S(2)}, u32[]{:S(2)}) async-start(bf16[128,3,8,256]{0,3,1,2:T(8,128)(2,1)} %copy.106), calls=%async_computation | async-start | bytes 3145728 | tf_op jit(solution)/shard_map/all_to_all | solution.py:200
  457.1 71.6 %all-to-all-start.1 = ((bf16[8,2,16384]{2,1,0:T(2,128)(2,1)}), bf16[8,2,16384]{2,1,0:T(2,128)(2,1)}, u32[]{:S(2)}, u32[]{:S(2)}) async-start(bf16[8,2,16384]{2,1,0:T(2,128)(2,1)} %reshape.497), calls=%async_computation.1 | async-start | bytes 1048576 | tf_op jit(solution)/shard_map/all_to_all | solution.py:206
  528.8 54.0 %all-to-all-start.3 = ((bf16[1024,3,1,256]{3,1,2,0:T(4,128)(2,1)}), bf16[1024,3,1,256]{3,1,2,0:T(4,128)(2,1)S(1)}, u32[]{:S(2)}, u32[]{:S(2)}) async-start(bf16[1024,3,1,256]{3,1,2,0:T(4,128)(2,1)} %copy.114), calls=%async_computation.3 | async-start | bytes 4194304 | tf_op jit(solution)/shard_map/all_to_all | solution.py:258
  582.8 19.5 %all-to-all-start.5 = ((bf16[128,4,8,64]{0,3,1,2:T(8,128)(2,1)}), bf16[128,4,8,64]{0,3,1,2:T(8,128)(2,1)}, u32[]{:S(2)}, u32[]{:S(2)}) async-start(bf16[128,4,8,64]{0,3,1,2:T(8,128)(2,1)} %copy.122), calls=%async_computation.6 | async-start | bytes 1048576 | tf_op jit(solution)/shard_map/all_to_all | solution.py:313
  602.3 41.3 %all-to-all-start.4 = ((bf16[128,8,768]{0,2,1:T(8,128)(2,1)}), bf16[128,8,768]{0,2,1:T(8,128)(2,1)S(1)}, u32[]{:S(2)}, u32[]{:S(2)}) async-start(bf16[128,8,768]{0,2,1:T(8,128)(2,1)} %bitcast.37), calls=%async_computation.4 | async-start | bytes 3145728 | tf_op jit(solution)/shard_map/all_to_all | solution.py:295
  605.9 591.2 %reduce-scatter.7.cloned.1.call-start = ((), (), s32[]{:S(2)}) async-start(), calls=%async_computation.19 | async-start | bytes 1310720 | tf_op jit(solution)/shard_map/reduce_scatter | solution.py:332
  612.0 585.8 %reduce-scatter.5.cloned.1.call-start = ((), (), s32[]{:S(2)}) async-start(), calls=%async_computation.17 | async-start | bytes 3932160 | tf_op jit(solution)/shard_map/reduce_scatter | solution.py:332
  644.3 107.0 %copy-start.10 = (bf16[128,2048]{1,0:T(8,128)(2,1)S(1)}, bf16[128,2048]{1,0:T(8,128)(2,1)}, u32[]{:S(2)}) copy-start(bf16[128,2048]{1,0:T(8,128)(2,1)} %fusion.64) | copy-start | bytes 1572868
  651.8 398.3 %copy-start.12 = (bf16[1,128,2048]{2,1,0:T(8,128)(2,1)S(1)}, bf16[1,128,2048]{2,1,0:T(8,128)(2,1)}, u32[]{:S(2)}) copy-start(bf16[1,128,2048]{2,1,0:T(8,128)(2,1)} %param.31) | copy-start | bytes 1572868
  651.8 546.5 %reduce-scatter.9.cloned.1.call-start = ((), (), s32[]{:S(2)}) async-start(), calls=%async_computation.21 | async-start | bytes 5242880 | tf_op jit(solution)/shard_map/reduce_scatter | solution.py:332
  1068.1 53.9 %copy-start.31 = (bf16[1024,2048]{1,0:T(8,128)(2,1)S(1)}, bf16[1024,2048]{1,0:T(8,128)(2,1)}, u32[]{:S(2)}) copy-start(bf16[1024,2048]{1,0:T(8,128)(2,1)} %all-gather.26.cloned.1.call-done) | copy-start | bytes 12582916
  1128.3 119.4 %reduce-scatter.11.cloned.1.call-start = ((), (), s32[]{:S(2)}) async-start(), calls=%async_computation.23 | async-start | bytes 5242880 | tf_op jit(solution)/shard_map/reduce_scatter | solution.py:332
  1136.4 54.5 %copy-start.30 = (bf16[1,1024,2048]{2,1,0:T(8,128)(2,1)S(1)}, bf16[1,1024,2048]{2,1,0:T(8,128)(2,1)}, u32[]{:S(2)}) copy-start(bf16[1,1024,2048]{2,1,0:T(8,128)(2,1)} %all-gather.36.cloned.1.call-done) | copy-start | bytes 12582916
  1196.9 52.7 %copy-start.28 = (bf16[512]{0:T(512)(128)(2,1)S(1)}, bf16[512]{0:T(512)(128)(2,1)}, u32[]{:S(2)}) copy-start(bf16[512]{0:T(512)(128)(2,1)} %param.24) | copy-start | bytes 3076
  1196.9 60.7 %copy-start.29 = (bf16[512]{0:T(512)(128)(2,1)S(1)}, bf16[512]{0:T(512)(128)(2,1)}, u32[]{:S(2)}) copy-start(bf16[512]{0:T(512)(128)(2,1)} %param.28) | copy-start | bytes 3076
  1196.9 67.9 %copy-start.4 = (bf16[1,128,2048]{2,1,0:T(8,128)(2,1)S(1)}, bf16[1,128,2048]{2,1,0:T(8,128)(2,1)}, u32[]{:S(2)}) copy-start(bf16[1,128,2048]{2,1,0:T(8,128)(2,1)} %param.18) | copy-start | bytes 1572868
  1197.0 67.9 %copy-start.8 = (bf16[128,8,1,256]{0,3,1,2:T(8,128)(2,1)S(1)}, bf16[128,8,1,256]{0,3,1,2:T(8,128)(2,1)}, u32[]{:S(2)}) copy-start(bf16[128,8,1,256]{0,3,1,2:T(8,128)(2,1)} %copy-done.7) | copy-start | bytes 1572868
  1197.0 88.2 %all-gather.30.cloned.1.call-start = ((), (), s32[]{:S(2)}) async-start(), calls=%async_computation.20 | async-start | bytes 2359296 | tf_op jit(solution)/shard_map/all_gather | solution.py:347
  1197.7 201.9 %all-gather.28.cloned.1.call-start = ((), (), s32[]{:S(2)}) async-start(), calls=%async_computation.18 | async-start | bytes 7077888 | tf_op jit(solution)/shard_map/all_gather | solution.py:344
  1198.3 229.7 %all-gather.32.cloned.1.call-start = ((), (), s32[]{:S(2)}) async-start(), calls=%async_computation.22 | async-start | bytes 9437184 | tf_op jit(solution)/shard_map/all_gather | solution.py:350
  1199.1 310.9 %all-gather.34.cloned.1.call-start = ((), (), s32[]{:S(2)}) async-start(), calls=%async_computation.24 | async-start | bytes 9437184 | tf_op jit(solution)/shard_map/all_gather | solution.py:353
  1307.2 78.0 %copy-start.6 = (bf16[128,8192]{1,0:T(8,128)(2,1)S(1)}, bf16[128,8192]{1,0:T(8,128)(2,1)}, u32[]{:S(2)}) copy-start(bf16[128,8192]{1,0:T(8,128)(2,1)} %get-tuple-element.254) | copy-start | bytes 6291460
  1371.8 149.9 %copy-start.19 = (f32[512]{0:T(512)}, f32[512]{0:T(512)S(1)}, u32[]{:S(2)}) copy-start(f32[512]{0:T(512)S(1)} %convert_element_type.215) | copy-start | bytes 6148
  (30 other events, 277.4 us)
Sparse Core Ops, SparseCore 0:
  9.9 90.3 all-gather.19
  102.2 227.5 all-gather.17
  331.4 74.1 all-gather.35
  407.6 45.9 all-gather.25
  455.2 296.0 all-gather.21
  753.0 297.0 all-gather.23
  1053.6 27.9 reduce-scatter.6
  1085.1 43.8 reduce-scatter.4
  1132.6 52.5 reduce-scatter.8
  1197.1 50.5 reduce-scatter.10
  1249.3 29.1 all-gather.29
  1279.9 64.8 all-gather.27
  1346.4 81.4 all-gather.31
  1429.4 80.4 all-gather.33
where the time goes:
time: 1540 us; the launch traced here: 1530 us
  waiting for transfers between devices  930 us (60%)
  blocking collectives  227 us (15%)
  matrix products  184 us (12%)
  other arithmetic  69 us (4%)
  local copies, waits for them, and re-layouts  68.4 us (4%)
  starting transfers between devices  27.6 us (2%)
  between operations  16.1 us (1%)
    all_gather x1, waiting for transfers between devices, body(): lax.all_gather(fc2_weight, 'fsdp', axis=0, tiled=True)  280 us
    all_gather x1, waiting for transfers between devices, body(): lax.all_gather(qkv_weight, 'fsdp', axis=0, tiled=True)  218 us
    all_gather x1, waiting for transfers between devices, body(): lax.all_gather(fc1_weight, 'fsdp', axis=0, tiled=True)  99.4 us
    all_gather x1, waiting for transfers between devices, body(): lax.all_gather(piece_down.astype(jnp.bfloat16), 'seq', axis=0, tiled=True)  69.5 us
    all_gather x1, waiting for transfers between devices, body(): lax.all_gather(dense_weight, 'fsdp', axis=0, tiled=True)  60.9 us
    unnamed x2, blocking collectives  59.4 us
    all_to_all x1, waiting for transfers between devices, body(): lax.all_to_all(outgoing, 'seq', split_axis=2, concat_axis=0, tiled=True)  56.5 us
    dot_general x4, matrix products, contract_cols(): lax.dot_general(left_side, right_side, (((1,), (1,)), ((), ())), preferre...  56.2 us
  transfers between devices with their start and end apart: 20, of which 11 were waited for; matrix products, arithmetic and copies ran while one was open for 20% of the time, Pallas kernels for 0%

commit v1 on v0

v1 whole, which is shorter than its diff:
```python
import functools

import jax
import jax.numpy as jnp
from jax import lax
from jax.experimental import pallas as pl
from jax.experimental.pallas import tpu as pltpu
from jax.sharding import PartitionSpec as P

HEADS = 32
HEAD = 64
ROT = 32
EPS = 1e-05
DOC_SHIFT = 1023
LANES = 2 * HEAD
BF = jnp.bfloat16
F32 = jnp.float32


def dot(left, right):
    return lax.dot_general(left, right, (((1,), (0,)), ((), ())), preferred_element_type=F32)


def dot_nt(left, right):
    return lax.dot_general(left, right, (((1,), (1,)), ((), ())), preferred_element_type=F32)


def dot_tn(left, right):
    return lax.dot_general(left, right, (((0,), (0,)), ((), ())), preferred_element_type=F32)


def gelu_tanh(values_in):
    return jax.nn.gelu(values_in, approximate=True)


def turn(values, cos, sin_low, sin_high):
    half = ROT // 2
    return (
        values * cos
        - pltpu.roll(values, LANES - half, 1) * sin_low
        + pltpu.roll(values, half, 1) * sin_high
    )


def attention_kernel(
    rows, proj, grad_out, cos, sin_low, sin_high, seg_col, seg_row,
    out, grad_proj, qs, ks, vs, dk, dv,
):
    length = proj.shape[0]
    blocks = length // rows
    scale = HEAD**-0.5
    for i in range(blocks):
        r = slice(i * rows, (i + 1) * rows)
        c, lo, hi = cos[r, :], sin_low[r, :], sin_high[r, :]
        qs[r, :] = turn(proj[r, 0:LANES], c, lo, hi).astype(BF) * jnp.asarray(scale, BF)
        ks[r, :] = turn(proj[r, LANES : 2 * LANES], c, lo, hi).astype(BF)
        vs[r, :] = proj[r, 2 * LANES : 3 * LANES].astype(BF)
    lane = lax.broadcasted_iota(jnp.int32, (rows, LANES), 1)
    first = lane < HEAD
    zero = jnp.zeros((rows, LANES), BF)
    for i in reversed(range(blocks)):
        r = slice(i * rows, (i + 1) * rows)
        n = (i + 1) * rows
        place_q = i * rows + lax.broadcasted_iota(jnp.int32, (rows, n), 0)
        place_k = lax.broadcasted_iota(jnp.int32, (rows, n), 1)
        allowed = (place_k <= place_q) & (seg_col[r, :] == seg_row[:, 0:n])
        q2, g2 = qs[r, :], grad_out[r, :]
        k, v = ks[0:n, :], vs[0:n, :]
        o_parts, dq_parts = [], []
        for h in range(2):
            mine = first if h == 0 else ~first
            q = jnp.where(mine, q2, zero)
            g = jnp.where(mine, g2, zero)
            s = jnp.where(allowed, dot_nt(q, k), -1e30)
            e = jnp.exp(s - jnp.max(s, axis=-1, keepdims=True))
            p = e * (1.0 / jnp.sum(e, axis=-1, keepdims=True))
            pb = p.astype(BF)
            o_parts.append(dot(pb, v))
            dp = dot_nt(g, v)
            inner = jnp.sum(p * dp, axis=-1, keepdims=True)
            ds = (p * (dp - inner)).astype(BF)
            dq_parts.append(dot(ds, k))
            dk_new, dv_new = dot_tn(ds, q), dot_tn(pb, g)
            if i == blocks - 1 and h == 0:
                dk[...] = dk_new
                dv[...] = dv_new
            else:
                dk[0:n, :] += dk_new
                dv[0:n, :] += dv_new
        out[r, :] = jnp.where(first, o_parts[0], o_parts[1]).astype(BF)
        dq = (jnp.where(first, dq_parts[0], dq_parts[1]) * scale).astype(BF).astype(F32)
        c, lo, hi = cos[r, :], sin_low[r, :], sin_high[r, :]
        grad_proj[r, 0:LANES] = turn(dq, c, -lo, -hi).astype(BF)
    for i in range(blocks):
        r = slice(i * rows, (i + 1) * rows)
        c, lo, hi = cos[r, :], sin_low[r, :], sin_high[r, :]
        grad_k = dk[r, :].astype(BF).astype(F32)
        grad_proj[r, LANES : 2 * LANES] = turn(grad_k, c, -lo, -hi).astype(BF)
        grad_proj[r, 2 * LANES : 3 * LANES] = dv[r, :].astype(BF)


def attention(proj, grad_att, tables, segments):
    length = proj.shape[0]
    pairs = grad_att.shape[1] // LANES
    rows = 256
    whole = lambda shape: pl.BlockSpec(shape, lambda p: (0, 0))
    return pl.pallas_call(
        functools.partial(attention_kernel, rows),
        grid=(pairs,),
        out_shape=(
            jax.ShapeDtypeStruct((length, pairs * LANES), BF),
            jax.ShapeDtypeStruct((length, 3 * pairs * LANES), BF),
        ),
        in_specs=[
            pl.BlockSpec((length, 3 * LANES), lambda p: (0, p)),
            pl.BlockSpec((length, LANES), lambda p: (0, p)),
            whole((length, LANES)),
            whole((length, LANES)),
            whole((length, LANES)),
            whole((length, 1)),
            whole((1, length)),
        ],
        out_specs=(
            pl.BlockSpec((length, LANES), lambda p: (0, p)),
            pl.BlockSpec((length, 3 * LANES), lambda p: (0, p)),
        ),
        scratch_shapes=[pltpu.VMEM((length, LANES), BF)] * 3
        + [pltpu.VMEM((length, LANES), F32)] * 2,
        cost_estimate=pl.CostEstimate(
            flops=14 * pairs * length * length * LANES,
            bytes_accessed=pairs * length * LANES * 24,
            transcendentals=pairs * length * length,
        ),
    )(proj, grad_att, *tables, segments[:, None], segments[None, :])


def angle_tables(seg_row):
    length = seg_row.shape[0]
    position = jnp.arange(length, dtype=jnp.int32) + jnp.where(seg_row > 0, DOC_SHIFT, 0)
    half = ROT // 2
    inverse = 1.0 / 10000.0 ** (jnp.arange(0, ROT, 2, dtype=F32) / ROT)
    angles = position.astype(F32)[:, None] * inverse[None, :]
    cosine, sine = jnp.cos(angles), jnp.sin(angles)
    ones = jnp.ones((length, HEAD - ROT), F32)
    zeros = jnp.zeros((length, HEAD - ROT), F32)
    none = jnp.zeros((length, half), F32)
    cos = jnp.concatenate([cosine, cosine, ones] * 2, axis=1)
    low = jnp.concatenate([sine, none, zeros] * 2, axis=1)
    high = jnp.concatenate([none, sine, zeros] * 2, axis=1)
    return cos, low, high


def body(
    tokens,
    ln_gain,
    ln_bias,
    qkv_weight,
    qkv_bias,
    dense_weight,
    dense_bias,
    fc1_weight,
    fc1_bias,
    fc2_weight,
    fc2_bias,
    segments,
    positions,
    cotangent,
):
    S, F = lax.axis_size("seq"), lax.axis_size("fsdp")
    j, f = lax.axis_index("seq"), lax.axis_index("fsdp")
    tok, D = tokens.shape[1], tokens.shape[2]
    length = tok * S
    rows_d = D // F
    ff = fc1_weight.shape[1]
    cols_up = ff // S
    block_up = cols_up // F
    hp = HEADS // S
    pairs = hp // 2
    per_shard = HEADS // F
    spread = per_shard % S == 0
    slots = per_shard // S if spread else 0

    def heads_of(array, lead):
        shape = array.shape
        if spread:
            split = array.reshape(shape[:lead] + (F, S, slots) + shape[lead + 1 :])
            mine = lax.dynamic_index_in_dim(split, j, lead + 1, keepdims=False)
            return mine.reshape(shape[:lead] + (hp,) + shape[lead + 1 :])
        return lax.dynamic_slice_in_dim(array, j * hp, hp, lead)

    def qkv_cols(array):
        n = array.shape[0]
        mine = heads_of(array.reshape(n, 3, HEADS, HEAD), 2)
        return mine.reshape(n, 3, pairs, 2, HEAD).transpose(0, 2, 1, 3, 4).reshape(n, -1)

    small = jnp.concatenate([ln_gain, ln_bias, qkv_bias, dense_bias, fc1_bias, fc2_bias])
    small = lax.all_gather(small, "fsdp", axis=0)
    cuts, at = [], 0
    for piece in (ln_gain, ln_bias, qkv_bias, dense_bias, fc1_bias, fc2_bias):
        cuts.append(small[:, at : at + piece.shape[0]].reshape(-1).astype(F32))
        at += piece.shape[0]
    gain, shift, b_qkv, b_dense, b_up, b_down = cuts

    inputs = tokens[0].astype(F32)
    centre = jnp.mean(inputs, axis=-1, keepdims=True)
    variance = jnp.mean((inputs - centre) ** 2, axis=-1, keepdims=True)
    inv_std = lax.rsqrt(variance + EPS)
    standard = (inputs - centre) * inv_std
    normed_own = (standard * gain + shift).astype(BF)
    upstream_own = cotangent[0]
    normed = lax.all_gather(normed_own, "seq", axis=0, tiled=True)
    upstream = lax.all_gather(upstream_own, "seq", axis=0, tiled=True)

    up_own = lax.dynamic_index_in_dim(
        fc1_weight.reshape(rows_d, F, S, block_up), j, 2, keepdims=False
    ).reshape(rows_d, cols_up)
    w_up = lax.all_gather(up_own, "fsdp", axis=0, tiled=True)
    down_own = lax.dynamic_slice_in_dim(fc2_weight, j * block_up, block_up, 0)
    w_down = lax.all_gather(down_own, "fsdp", axis=0, tiled=True)
    w_qkv = lax.all_gather(qkv_cols(qkv_weight), "fsdp", axis=0, tiled=True)
    if spread:
        block_dense = slots * HEAD
        dense_own = lax.dynamic_slice_in_dim(dense_weight, j * block_dense, block_dense, 0)
        w_dense = lax.all_gather(dense_own, "fsdp", axis=0, tiled=True)
    else:
        w_dense = lax.dynamic_slice_in_dim(
            lax.all_gather(dense_weight, "fsdp", axis=0, tiled=True), j * hp * HEAD, hp * HEAD, 0
        )

    bias_up = lax.dynamic_index_in_dim(b_up.reshape(F, S, block_up), j, 1, keepdims=False)
    bias_up = bias_up.reshape(-1)
    bias_qkv = qkv_cols(b_qkv[None])[0]
    seg_row = segments[0]

    pre_act = dot(normed, w_up) + bias_up
    activated = gelu_tanh(pre_act).astype(BF)
    grad_act = dot_nt(upstream, w_down)
    grad_pre = jax.vjp(gelu_tanh, pre_act)[1](grad_act)[0].astype(BF)
    projected = dot(normed, w_qkv) + bias_qkv
    grad_att = dot_nt(upstream, w_dense).astype(BF)
    attended, grad_mixed = attention(projected, grad_att, angle_tables(seg_row), seg_row)

    partial_out = dot(attended, w_dense) + dot(activated, w_down)
    branches = lax.psum_scatter(partial_out.astype(BF), "seq", scatter_dimension=0, tiled=True)
    result = (inputs + branches.astype(F32) + (b_dense + b_down)).astype(BF)

    partial_normed = dot_nt(grad_mixed, w_qkv) + dot_nt(grad_pre, w_up)
    grad_normed = lax.psum_scatter(
        partial_normed.astype(BF), "seq", scatter_dimension=0, tiled=True
    ).astype(F32)
    scaled = grad_normed * gain
    grad_inputs = upstream_own.astype(F32) + inv_std * (
        scaled
        - jnp.mean(scaled, axis=-1, keepdims=True)
        - standard * jnp.mean(scaled * standard, axis=-1, keepdims=True)
    )

    def summed(left, right):
        return lax.psum_scatter(
            dot_tn(left, right).astype(BF), "fsdp", scatter_dimension=0, tiled=True
        )

    piece_down = summed(activated, upstream)
    piece_up = summed(normed, grad_pre)
    piece_qkv = summed(normed, grad_mixed)
    grad_down = lax.all_gather(piece_down, "seq", axis=0, tiled=True).astype(F32)
    grad_up = (
        lax.all_gather(piece_up, "seq", axis=0)
        .reshape(S, rows_d, F, block_up)
        .transpose(1, 2, 0, 3)
        .reshape(rows_d, ff)
        .astype(F32)
    )

    def to_heads(array, lead):
        shape = array.shape
        if spread:
            split = array.reshape(shape[: 1 + lead] + (F, slots) + shape[2 + lead :])
            moved = jnp.moveaxis(split, 0, lead + 1)
        else:
            moved = jnp.moveaxis(array, 0, lead)
        return moved.reshape(shape[1 : 1 + lead] + (HEADS,) + shape[2 + lead :])

    def from_qkv_cols(gathered):
        n = gathered.shape[1]
        split = gathered.reshape(S, n, pairs, 3, 2, HEAD).transpose(0, 1, 3, 2, 4, 5)
        return to_heads(split.reshape(S, n, 3, hp, HEAD), 2).reshape(n, -1)

    grad_qkv = from_qkv_cols(lax.all_gather(piece_qkv, "seq", axis=0)).astype(F32)
    if spread:
        piece_dense = summed(attended, upstream)
        grad_dense = lax.all_gather(piece_dense, "seq", axis=0, tiled=True).astype(F32)
    else:
        part = lax.all_gather(dot_tn(attended, upstream).astype(BF), "seq", axis=0, tiled=True)
        grad_dense = lax.psum_scatter(part, "fsdp", scatter_dimension=0, tiled=True).astype(F32)

    ln_terms = jnp.concatenate(
        [jnp.sum(grad_normed * standard, axis=0), jnp.sum(grad_normed, axis=0)]
    )
    ln_terms = lax.psum_scatter(ln_terms, "seq", scatter_dimension=0, tiled=True)
    out_term = jnp.sum(upstream.astype(F32), axis=0)
    out_term = lax.dynamic_slice_in_dim(out_term, j * (D // S), D // S, 0)
    up_term = jnp.sum(grad_pre.astype(F32), axis=0)
    qkv_term = jnp.sum(grad_mixed.astype(F32), axis=0)
    terms = lax.psum(jnp.concatenate([ln_terms, out_term, up_term, qkv_term]), "fsdp")
    terms = lax.all_gather(terms, "seq", axis=0)
    n_ln = 2 * D // S
    n_out = n_ln + D // S
    n_up = n_out + cols_up
    ln_full = terms[:, :n_ln].reshape(2, F, rows_d)
    ln_mine = lax.dynamic_index_in_dim(ln_full, f, 1, keepdims=False)
    out_full = terms[:, n_ln:n_out].reshape(F, rows_d)
    out_mine = lax.dynamic_index_in_dim(out_full, f, 0, keepdims=False)
    up_full = terms[:, n_out:n_up].reshape(S, F, block_up)
    up_mine = lax.dynamic_index_in_dim(up_full, f, 1, keepdims=False).reshape(-1)
    qkv_full = from_qkv_cols(terms[:, n_up:][:, None]).reshape(F, -1)
    qkv_mine = lax.dynamic_index_in_dim(qkv_full, f, 0, keepdims=False)
    return (
        result[None],
        grad_inputs[None],
        ln_mine[0],
        ln_mine[1],
        grad_qkv,
        qkv_mine,
        grad_dense,
        out_mine,
        grad_up,
        up_mine,
        grad_down,
        out_mine,
    )


def solution(mesh):
    row, mat = P("fsdp"), P("fsdp", None)
    act = P("fsdp", "seq", None)
    return jax.shard_map(
        body,
        mesh=mesh,
        in_specs=(
            act, row, row, mat, row, mat, row, mat, row, mat, row, mat, P("fsdp", "seq"), act,
        ),
        out_specs=(act, act, row, row, mat, row, mat, row, mat, row, mat, row),
        check_vma=False,
    )
```

time: 1540 us -> 872 us (0.57)
  waiting for transfers between devices: 930 us -> 477 us
  blocking collectives: 227 us -> 67.1 us
  local copies, waits for them, and re-layouts: 68.4 us -> 166 us
  matrix products: 184 us -> 87.2 us
  other arithmetic: 69 us -> 27.2 us
  starting transfers between devices: 27.6 us -> 1.44 us
  Pallas kernels: 0 us -> 21.5 us
    all_gather x10, waiting for transfers between devices: 747 us -> 294 us  [the longest x1 52.7 us: body(): lax.all_gather(piece_qkv, 'seq', axis=0)]
    reduce_scatter x4 -> x6, waiting for transfers between devices: 48.6 us -> 182 us  [the longest x4 135 us: summed(): lax.psum_scatter(dot_tn(left, right).astype(BF), 'fsdp', scatter_dimensio...]
    all_to_all x6 -> x0, waiting for transfers between devices: 129 us -> none  [the longest x1 56.5 us: body(): lax.all_to_all(outgoing, 'seq', split_axis=2, concat_axis=0, tiled=True)]
    all_to_all x2 -> x0, blocking collectives: 107 us -> none  [the longest x1 53.7 us: body(): lax.all_to_all(grad_pre.reshape(tok_len, seq_count, col_up), 'seq', split...]
    dot_general x26 -> x12, matrix products: 184 us -> 87.2 us  [the longest x4 30.2 us: dot(): lax.dot_general(left, right, (((1,), (0,)), ((), ())), preferred_element_...]
    unnamed x86 -> x62, local copies, waits for them, and re-layouts: 11.8 us -> 79.2 us
    convert_element_type x4 -> x6, local copies, waits for them, and re-layouts: 9.98 us -> 71 us  [the longest x3 38.7 us: body(): from_qkv_cols(lax.all_gather(piece_qkv, 'seq', axis=0)).astype(F32)]
    all_gather x7 -> x2, blocking collectives: 60.9 us -> 23.9 us  [the longest x1 14 us: body(): terms = lax.all_gather(terms, 'seq', axis=0)]
  transfers between devices with their start and end apart: 20 -> 16, of which waited for: 11 -> 14; matrix products, arithmetic and copies ran while one was open for 20% -> 31% of each run, Pallas kernels for 0% -> 2%
where the time goes in v1:
time: 872 us; the launch traced here: 863 us
  waiting for transfers between devices  477 us (55%)
  local copies, waits for them, and re-layouts  166 us (19%)
  matrix products  87.2 us (10%)
  blocking collectives  67.1 us (8%)
  other arithmetic  27.2 us (3%)
  Pallas kernels  21.5 us (2%)
  between operations  15.5 us (2%)
    reduce_scatter x4, waiting for transfers between devices, summed(): lax.psum_scatter(dot_tn(left, right).astype(BF), 'fsdp', scatter_dimensio...  135 us
    unnamed x62, local copies, waits for them, and re-layouts  79.2 us
    all_gather x1, waiting for transfers between devices, body(): lax.all_gather(piece_qkv, 'seq', axis=0)  52.7 us
    all_gather x1, waiting for transfers between devices, body(): normed = lax.all_gather(normed_own, 'seq', axis=0, tiled=True)  48.9 us
    reduce_scatter x1, waiting for transfers between devices, body(): lax.psum_scatter(partial_normed.astype(BF), 'seq', scatter_dimension=0, t...  47.9 us
    all_gather x1, waiting for transfers between devices, body(): w_down = lax.all_gather(down_own, 'fsdp', axis=0, tiled=True)  44.9 us
    all_gather x1, waiting for transfers between devices, body(): w_qkv = lax.all_gather(qkv_cols(qkv_weight), 'fsdp', axis=0, tiled=True)  40.4 us
    convert_element_type x3, local copies, waits for them, and re-layouts, body(): from_qkv_cols(lax.all_gather(piece_qkv, 'seq', axis=0)).astype(F32)  38.7 us
  transfers between devices with their start and end apart: 16, of which 14 were waited for; matrix products, arithmetic and copies ran while one was open for 31% of the time, Pallas kernels for 2%

profile of v1, /device:TPU:0, one launch (start us, length us, event | category | flops | bytes accessed | tf_op | source)
XLA Modules:
  0.0 863.1 jit_solution(14509016277306161963)
XLA Ops:
  10.4 8.6 %copy.49 = bf16[512,6144]{0,1:T(8,128)(2,1)} copy(bf16[512,6144]{1,0:T(8,128)(2,1)} %param.17) | data formatting | bytes 12582912 | tf_op args[3]
  22.4 9.8 %all-gather.4 = bf16[4,1,5632]{2,1,0:T(2,128)(2,1)S(1)} all-gather(bf16[1,1,5632]{2,1,0:T(2,128)(2,1)S(1)} %reshape.188), channel_id=2, replica_groups=mesh['seq'=8,'fsdp'=4] {'fsdp'}, dimensions={0}, use_global_device_ids=true | all-gather | bytes 56320 | tf_op jit(solution)/shard_map/all_gather | solution.py:197
  34.0 11.9 %copy.55 = bf16[512,8192]{0,1:T(8,128)(2,1)} copy(bf16[512,8192]{1,0:T(8,128)(2,1)} %param.21) | data formatting | bytes 16777216 | tf_op args[7]
  59.3 28.9 %all-gather.31.cloned.1.call-done = bf16[1,1024,2048]{2,1,0:T(8,128)(2,1)} async-done(((bf16[1,128,2048]{2,1,0:T(8,128)(2,1)}), bf16[1,1024,2048]{2,1,0:T(8,128)(2,1)}) %all-gather.31.cloned.1.call-update) | async-done | bytes 4194320 | tf_op jit(solution)/shard_map/all_gather | solution.py:212
  92.8 40.4 %all-gather.19.cloned.1.call-done = bf16[2048,768]{0,1:T(8,128)(2,1)} async-done(((bf16[512,768]{0,1:T(8,128)(2,1)}), bf16[2048,768]{0,1:T(8,128)(2,1)}) %all-gather.19.cloned.1.call-update) | async-done | bytes 3145744 | tf_op jit(solution)/shard_map/all_gather | solution.py:220
  133.1 48.9 %all-gather.17.cloned.1.call-done = bf16[1024,2048]{1,0:T(8,128)(2,1)} async-done(((bf16[128,2048]{1,0:T(8,128)(2,1)}), bf16[1024,2048]{1,0:T(8,128)(2,1)}) %all-gather.17.cloned.1.call-update) | async-done | bytes 4194320 | tf_op jit(solution)/shard_map/all_gather | solution.py:211
  190.3 21.5 %shard_map.220 = (bf16[1024,256]{1,0:T(8,128)(2,1)}, bf16[1024,768]{1,0:T(8,128)(2,1)}) custom-call(f32[1024,768]{1,0:T(8,128)} %convolution_add_fusion.proj, bf16[1024,256]{1,0:T(8,128)(2,1)} %fusion.38.grad_out, f32[1024,128]{1,0:T(8,128)} %concatenate.19.cos, f32[1024,128]{1,0:T(8,128)} %concatenate.20.sin_low, f32[1024,128]{1,0:T(8,128)} %concatenate.21.sin_high, ...), custom_call_target="tpu_custom_call" | custom-call | flops 3758096384 | bytes 6291456 | tf_op jit(solution)/shard_map/pallas_call | solution.py:107
  224.5 11.1 %all-gather.23.cloned.1.call-done = bf16[2048,1024]{0,1:T(8,128)(2,1)} async-done(((bf16[512,1024]{0,1:T(8,128)(2,1)}), bf16[2048,1024]{0,1:T(8,128)(2,1)}) %all-gather.23.cloned.1.call-update) | async-done | bytes 4194320 | tf_op jit(solution)/shard_map/all_gather | solution.py:217
  235.6 10.0 %fusion.54 = f32[1024,1024]{1,0:T(8,128)} fusion(bf16[1024,2048]{1,0:T(8,128)(2,1)} %all-gather.17.cloned.1.call-done, bf16[2048,1024]{0,1:T(8,128)(2,1)} %all-gather.23.cloned.1.call-done), kind=kOutput, calls=%fused_computation.94 | convolution fusion | flops 4294967296 | bytes 12582912 | tf_op jit(solution)/shard_map/dot_general | solution.py:21
  245.6 44.9 %all-gather.25.cloned.1.call-done = bf16[1024,2048]{1,0:T(8,128)(2,1)} async-done(((bf16[256,2048]{1,0:T(8,128)(2,1)}), bf16[1024,2048]{1,0:T(8,128)(2,1)}) %all-gather.25.cloned.1.call-update) | async-done | bytes 4194320 | tf_op jit(solution)/shard_map/all_gather | solution.py:219
  290.5 11.7 %convert_reduce_fusion.1 = (f32[1024]{0:T(1024)S(1)}, bf16[1024,1024]{1,0:T(8,128)(2,1)S(1)}) fusion(f32[1024,1024]{1,0:T(8,128)} %fusion.54, f32[1024]{0:T(1024)S(1)} %bitcast.208, bf16[1024,2048]{1,0:T(8,128)(2,1)} %all-gather.25.cloned.1.call-done, bf16[1,1024,2048]{2,1,0:T(8,128)(2,1)} %all-gather.31.cloned.1.call-done), kind=kOutput, calls=%fused_computation.25 | convolution fusion | flops 4319083520 | bytes 14688256 | tf_op jit(solution)/shard_map/dot_general | solution.py:25
  310.0 10.8 %fusion.18 = bf16[1024,2048]{1,0:T(8,128)(2,1)} fusion(bf16[1,1024,2048]{2,1,0:T(8,128)(2,1)} %all-gather.31.cloned.1.call-done, f32[1024,1024]{1,0:T(8,128)} %fusion.54, f32[1024]{0:T(1024)S(1)} %bitcast.209), kind=kOutput, calls=%fused_computation.27 | convolution fusion | flops 4307550208 | bytes 12587008 | tf_op jit(solution)/shard_map/dot_general | solution.py:29
  345.6 22.6 %reduce-scatter.11.cloned.1.call-done = bf16[512,768]{1,0:T(8,128)(2,1)} async-done(((bf16[2048,768]{1,0:T(8,128)(2,1)}), bf16[512,768]{1,0:T(8,128)(2,1)}) %reduce-scatter.11.cloned.1.call-update) | async-done | bytes 786448 | tf_op jit(solution)/shard_map/reduce_scatter | solution.py:259
  368.3 56.1 %reduce-scatter.15.cloned.1.call-done = bf16[512,1024]{1,0:T(8,128)(2,1)} async-done(((bf16[2048,1024]{1,0:T(8,128)(2,1)}), bf16[512,1024]{1,0:T(8,128)(2,1)}) %reduce-scatter.15.cloned.1.call-update) | async-done | bytes 1048592 | tf_op jit(solution)/shard_map/reduce_scatter | solution.py:259
  424.5 55.4 %reduce-scatter.17.cloned.1.call-done = bf16[256,2048]{1,0:T(8,128)(2,1)} async-done(((bf16[1024,2048]{1,0:T(8,128)(2,1)}), bf16[256,2048]{1,0:T(8,128)(2,1)}) %reduce-scatter.17.cloned.1.call-update) | async-done | bytes 1048592 | tf_op jit(solution)/shard_map/reduce_scatter | solution.py:259
  484.4 26.3 %all-gather.27.cloned.1.call-done = bf16[512,2048]{1,0:T(8,128)(2,1)} async-done(((bf16[64,2048]{1,0:T(8,128)(2,1)}), bf16[512,2048]{1,0:T(8,128)(2,1)}) %all-gather.27.cloned.1.call-update) | async-done | bytes 2097168 | tf_op jit(solution)/shard_map/all_gather | solution.py:292
  514.8 47.9 %reduce-scatter.9.cloned.1.call-done = bf16[128,2048]{1,0:T(8,128)(2,1)} async-done(((bf16[1024,2048]{1,0:T(8,128)(2,1)}), bf16[128,2048]{1,0:T(8,128)(2,1)}) %reduce-scatter.9.cloned.1.call-update) | async-done | bytes 524304 | tf_op jit(solution)/shard_map/reduce_scatter | solution.py:248
  564.3 27.3 %all-reduce = f32[4096]{0:T(1024)S(1)} all-reduce(f32[4096]{0:T(1024)S(1)} %pad_maximum_fusion), channel_id=8, replica_groups=mesh['seq'=8,'fsdp'=4] {'seq'}, use_global_device_ids=true, to_apply=%region_8.9.clone | all-reduce | flops 4096 | bytes 32768
  591.6 16.0 %psum.7 = f32[1,2560]{1,0:T(1,128)S(1)} all-reduce(f32[1,2560]{1,0:T(1,128)S(1)} %all_gather.56), channel_id=1, replica_groups=mesh['seq'=8,'fsdp'=4] {'fsdp'}, use_global_device_ids=true, to_apply=%region_12.13 | all-reduce | flops 2560 | bytes 20480 | tf_op jit(solution)/shard_map/psum | solution.py:305
  607.6 14.0 %all-gather.5 = f32[8,1,2560]{2,1,0:T(1,128)S(1)} all-gather(f32[1,1,2560]{2,1,0:T(1,128)S(1)} %bitcast.199), channel_id=1, replica_groups=mesh['seq'=8,'fsdp'=4] {'seq'}, dimensions={0}, use_global_device_ids=true | all-gather | bytes 92160 | tf_op jit(solution)/shard_map/all_gather | solution.py:306
  626.8 52.7 %all-gather.33.cloned.1.call-done = bf16[4096,768]{1,0:T(8,128)(2,1)} async-done(((bf16[512,768]{1,0:T(8,128)(2,1)}), bf16[4096,768]{1,0:T(8,128)(2,1)}) %all-gather.33.cloned.1.call-update) | async-done | bytes 6291472 | tf_op jit(solution)/shard_map/all_gather | solution.py:289
  679.5 9.7 %copy.56 = f32[4096,768]{0,1:T(8,128)} copy(bf16[4096,768]{1,0:T(8,128)(2,1)} %all-gather.33.cloned.1.call-done) | data formatting | bytes 18874368 | tf_op jit(solution)/shard_map/convert_element_type | solution.py:289
  689.2 22.1 %copy.70 = f32[96,8,8,512]{3,2,1,0:T(8,128)} copy(f32[96,8,8,512]{3,1,2,0:T(8,128)} %bitcast.173) | data formatting | bytes 25165824
  711.3 16.7 %copy.57 = f32[8,512,3,2,2,64]{1,5,4,3,2,0:T(8,128)} copy(f32[8,512,3,2,2,64]{1,0,5,4,2,3:T(8,128)} %bitcast.174) | data formatting | bytes 25165824 | tf_op jit(solution)/shard_map/convert_element_type | solution.py:289
  728.0 12.3 %copy.58 = f32[512,3,4,8,1,64]{0,5,3,2,1,4:T(8,128)} copy(f32[512,3,4,8,1,64]{0,5,2,1,3,4:T(8,128)} %bitcast.175) | data formatting | bytes 25165824 | tf_op jit(solution)/shard_map/convert_element_type | solution.py:289
  740.4 12.6 %copy.61 = f32[512,6144]{1,0:T(8,128)} copy(f32[512,6144]{0,1:T(8,128)} %bitcast.176) | data formatting | bytes 25165824
  753.0 8.7 %all-gather.35.cloned.1.call-done = bf16[4096,1024]{1,0:T(8,128)(2,1)} async-done(((bf16[512,1024]{1,0:T(8,128)(2,1)}), bf16[4096,1024]{1,0:T(8,128)(2,1)}) %all-gather.35.cloned.1.call-update) | async-done | bytes 8388624 | tf_op jit(solution)/shard_map/all_gather | solution.py:268
  761.7 16.7 %reshape.177 = f32[8,512,4,256]{3,2,1,0:T(4,128)} reshape(bf16[4096,1024]{1,0:T(8,128)(2,1)} %all-gather.35.cloned.1.call-done) | data formatting | bytes 25165824 | tf_op jit(solution)/shard_map/convert_element_type | solution.py:272
  778.4 15.5 %copy.60 = f32[512,4,8,256]{3,2,1,0:T(8,128)S(1)} copy(f32[512,4,8,256]{3,1,0,2:T(4,128)} %bitcast.171) | data formatting | bytes 33554432 | tf_op jit(solution)/shard_map/convert_element_type | solution.py:272
  793.9 18.0 %copy.71 = f32[64,8,32,256]{3,1,2,0:T(8,128)} copy(f32[64,8,32,256]{3,2,1,0:T(8,128)S(1)} %bitcast.172) | data formatting | bytes 33554432
  811.9 31.8 %all-gather.29.cloned.1.call-done = bf16[2048,2048]{1,0:T(8,128)(2,1)} async-done(((bf16[256,2048]{1,0:T(8,128)(2,1)}), bf16[2048,2048]{1,0:T(8,128)(2,1)}) %all-gather.29.cloned.1.call-update) | async-done | bytes 8388624 | tf_op jit(solution)/shard_map/all_gather | solution.py:266
  843.7 11.8 %convert_element_type.196 = f32[2048,2048]{1,0:T(8,128)} convert(bf16[2048,2048]{1,0:T(8,128)(2,1)} %all-gather.29.cloned.1.call-done) | non-fusion elementwise | flops 4194304 | bytes 25165824 | tf_op jit(solution)/shard_map/convert_element_type | solution.py:266
  (155 shorter events, 94.7 us)
Async XLA Ops:
  7.2 52.1 %all-gather.21.cloned.1.call-start = ((), (), s32[]{:S(2)}) async-start(), calls=%async_computation.8 | async-start | bytes 1310720 | tf_op jit(solution)/shard_map/all_gather | solution.py:224
  9.5 78.7 %all-gather.31.cloned.1.call-start = ((), (), s32[]{:S(2)}) async-start(), calls=%async_computation.19 | async-start | bytes 4718592 | tf_op jit(solution)/shard_map/all_gather | solution.py:212
  10.3 122.9 %all-gather.19.cloned.1.call-start = ((), (), s32[]{:S(2)}) async-start(), calls=%async_computation.7 | async-start | bytes 3932160 | tf_op jit(solution)/shard_map/all_gather | solution.py:220
  10.3 11.0 %copy-start.12 = (bf16[512]{0:T(512)(128)(2,1)S(1)}, bf16[512]{0:T(512)(128)(2,1)}, u32[]{:S(2)}) copy-start(bf16[512]{0:T(512)(128)(2,1)} %param.15) | copy-start | bytes 3076
  10.3 11.3 %copy-start.13 = (bf16[512]{0:T(512)(128)(2,1)S(1)}, bf16[512]{0:T(512)(128)(2,1)}, u32[]{:S(2)}) copy-start(bf16[512]{0:T(512)(128)(2,1)} %param.16) | copy-start | bytes 3076
  10.3 11.5 %copy-start.9 = (bf16[1536]{0:T(1024)(128)(2,1)S(1)}, bf16[1536]{0:T(1024)(128)(2,1)}, u32[]{:S(2)}) copy-start(bf16[1536]{0:T(1024)(128)(2,1)} %param.18) | copy-start | bytes 9220
  10.4 11.7 %copy-start.14 = (bf16[512]{0:T(512)(128)(2,1)S(1)}, bf16[512]{0:T(512)(128)(2,1)}, u32[]{:S(2)}) copy-start(bf16[512]{0:T(512)(128)(2,1)} %param.20) | copy-start | bytes 3076
  10.4 12.0 %copy-start.10 = (bf16[2048]{0:T(1024)(128)(2,1)S(1)}, bf16[2048]{0:T(1024)(128)(2,1)}, u32[]{:S(2)}) copy-start(bf16[2048]{0:T(1024)(128)(2,1)} %param.22) | copy-start | bytes 12292
  10.4 11.9 %copy-start.11 = (bf16[512]{0:T(512)(128)(2,1)S(1)}, bf16[512]{0:T(512)(128)(2,1)}, u32[]{:S(2)}) copy-start(bf16[512]{0:T(512)(128)(2,1)} %param.24) | copy-start | bytes 3076
  19.0 13.2 %copy-start.2 = (bf16[1,128,2048]{2,1,0:T(8,128)(2,1)S(1)}, bf16[1,128,2048]{2,1,0:T(8,128)(2,1)}, u32[]{:S(2)}) copy-start(bf16[1,128,2048]{2,1,0:T(8,128)(2,1)} %param.14) | copy-start | bytes 1572868
  21.3 160.8 %all-gather.17.cloned.1.call-start = ((), (), s32[]{:S(2)}) async-start(), calls=%async_computation.6 | async-start | bytes 4718592 | tf_op jit(solution)/shard_map/all_gather | solution.py:211
  33.9 201.6 %all-gather.23.cloned.1.call-start = ((), (), s32[]{:S(2)}) async-start(), calls=%async_computation.9 | async-start | bytes 5242880 | tf_op jit(solution)/shard_map/all_gather | solution.py:217
  48.2 242.2 %all-gather.25.cloned.1.call-start = ((), (), s32[]{:S(2)}) async-start(), calls=%async_computation.10 | async-start | bytes 5242880 | tf_op jit(solution)/shard_map/all_gather | solution.py:219
  50.7 270.6 %reduce-scatter.13.cloned.1.call-start = ((), (), s32[]{:S(2)}) async-start(), calls=%async_computation.14 | async-start | bytes 1310720 | tf_op jit(solution)/shard_map/reduce_scatter | solution.py:259
  216.7 151.5 %reduce-scatter.11.cloned.1.call-start = ((), (), s32[]{:S(2)}) async-start(), calls=%async_computation.13 | async-start | bytes 3932160 | tf_op jit(solution)/shard_map/reduce_scatter | solution.py:259
  224.2 200.2 %reduce-scatter.15.cloned.1.call-start = ((), (), s32[]{:S(2)}) async-start(), calls=%async_computation.16 | async-start | bytes 5242880 | tf_op jit(solution)/shard_map/reduce_scatter | solution.py:259
  290.5 13.1 %copy-start.16 = (bf16[1024,2048]{1,0:T(8,128)(2,1)S(1)}, bf16[1024,2048]{1,0:T(8,128)(2,1)}, u32[]{:S(2)}) copy-start(bf16[1024,2048]{1,0:T(8,128)(2,1)} %all-gather.17.cloned.1.call-done) | copy-start | bytes 12582916
  309.8 170.1 %reduce-scatter.17.cloned.1.call-start = ((), (), s32[]{:S(2)}) async-start(), calls=%async_computation.17 | async-start | bytes 5242880 | tf_op jit(solution)/shard_map/reduce_scatter | solution.py:259
  320.8 189.8 %all-gather.27.cloned.1.call-start = ((), (), s32[]{:S(2)}) async-start(), calls=%async_computation.15 | async-start | bytes 2359296 | tf_op jit(solution)/shard_map/all_gather | solution.py:292
  321.5 241.2 %reduce-scatter.9.cloned.1.call-start = ((), (), s32[]{:S(2)}) async-start(), calls=%async_computation.12 | async-start | bytes 4718592 | tf_op jit(solution)/shard_map/reduce_scatter | solution.py:248
  321.6 5.5 copy-start.15
  321.6 5.5 copy-start.19
  333.1 9.0 %copy-start.6 = (bf16[1024,256]{1,0:T(8,128)(2,1)S(1)}, bf16[1024,256]{1,0:T(8,128)(2,1)}, u32[]{:S(2)}) copy-start(bf16[1024,256]{1,0:T(8,128)(2,1)} %get-tuple-element.14) | copy-start | bytes 1572868
  333.1 290.6 %reduce-scatter.7.cloned.1.call-start = ((), (), s32[]{:S(2)}) async-start(), calls=%async_computation.11 | async-start | bytes 4718592 | tf_op jit(solution)/shard_map/reduce_scatter | solution.py:244
  333.6 8.5 copy-start.5
  345.5 134.4 %copy-start.17 = (u32[32]{0:T(128)S(1)}, u32[32]{0:T(128)}, u32[]{:S(2)}) copy-start(u32[32]{0:T(128)} %constant.94) | copy-start | bytes 388
  345.6 333.9 %all-gather.33.cloned.1.call-start = ((), (), s32[]{:S(2)}) async-start(), calls=%async_computation.20 | async-start | bytes 7077888 | tf_op jit(solution)/shard_map/all_gather | solution.py:289
  368.3 393.4 %all-gather.35.cloned.1.call-start = ((), (), s32[]{:S(2)}) async-start(), calls=%async_computation.21 | async-start | bytes 9437184 | tf_op jit(solution)/shard_map/all_gather | solution.py:268
  424.4 419.2 %all-gather.29.cloned.1.call-start = ((), (), s32[]{:S(2)}) async-start(), calls=%async_computation.18 | async-start | bytes 9437184 | tf_op jit(solution)/shard_map/all_gather | solution.py:266
  484.3 139.4 %copy-start.3 = (bf16[1,128,2048]{2,1,0:T(8,128)(2,1)S(1)}, bf16[1,128,2048]{2,1,0:T(8,128)(2,1)}, u32[]{:S(2)}) copy-start(bf16[1,128,2048]{2,1,0:T(8,128)(2,1)} %param.26) | copy-start | bytes 1572868
  621.7 233.8 %copy-start.8 = (f32[1,512]{1,0:T(1,128)}, f32[1,512]{1,0:T(1,128)S(1)}, u32[]{:S(2)}) copy-start(f32[1,512]{1,0:T(1,128)S(1)} %constant_dynamic-slice_fusion.1) | copy-start | bytes 6148
  843.7 12.4 %copy-start.1 = (bf16[512,2048]{1,0:T(8,128)(2,1)S(1)}, bf16[512,2048]{1,0:T(8,128)(2,1)}, u32[]{:S(2)}) copy-start(bf16[512,2048]{1,0:T(8,128)(2,1)} %param.19) | copy-start | bytes 6291460
  (4 other events, 12.7 us)
Sparse Core Ops, SparseCore 0:
  10.4 29.2 all-gather.20
  41.3 46.8 all-gather.30
  90.6 42.5 all-gather.18
  135.2 46.8 all-gather.16
  184.3 51.2 all-gather.22
  237.9 52.5 all-gather.24
  293.3 27.9 reduce-scatter.12
  324.3 43.8 reduce-scatter.10
  371.8 52.5 reduce-scatter.14
  427.2 52.5 reduce-scatter.16
  481.5 29.1 all-gather.26
  513.4 49.3 reduce-scatter.8
  565.6 48.8 reduce-scatter.6
  616.0 63.4 all-gather.32
  681.0 80.6 all-gather.34
  763.1 80.5 all-gather.28

commit v2 on v1

--- a/solution.py
+++ b/solution.py
@@ -6,6 +6,7 @@
 from jax.experimental import pallas as pl
 from jax.experimental.pallas import tpu as pltpu
 from jax.sharding import PartitionSpec as P
+
 
 HEADS = 32
 HEAD = 64
@@ -150,6 +151,580 @@
     return cos, low, high
 
 
+MESH = pl.DeviceIdType.MESH
+
+
+def remote(src, dst, send, recv, device):
+    return pltpu.make_async_remote_copy(
+        src_ref=src, dst_ref=dst, send_sem=send, recv_sem=recv, device_id=device,
+        device_id_type=MESH,
+    )
+
+
+class Place:
+    def __init__(self, S, F):
+        self.S, self.F, self.Q = S, F, S // 2
+        self.j, self.f = lax.axis_index("seq"), lax.axis_index("fsdp")
+        self.q, self.c = self.j // 2, lax.rem(self.j, 2)
+        self.partner = 2 * self.q + 1 - self.c
+
+    def greet(self, over_fsdp, over_seq):
+        barrier = pltpu.get_barrier_semaphore()
+        count = 0
+        if over_fsdp:
+            for k in range(1, self.F):
+                pl.semaphore_signal(
+                    barrier, inc=1, device_id=(self.j, lax.rem(self.f + k, self.F)),
+                    device_id_type=MESH,
+                )
+            count = self.F - 1
+        if over_seq:
+            pl.semaphore_signal(
+                barrier, inc=1, device_id=(self.partner, self.f), device_id_type=MESH
+            )
+
+            @pl.when(self.q > 0)
+            def _():
+                pl.semaphore_signal(
+                    barrier, inc=1, device_id=(self.j - 2, self.f), device_id_type=MESH
+                )
+
+            @pl.when(self.q < self.Q - 1)
+            def _():
+                pl.semaphore_signal(
+                    barrier, inc=1, device_id=(self.j + 2, self.f), device_id_type=MESH
+                )
+
+            count += 1 + (self.q + self.Q - 1) // self.Q + (2 * self.Q - 2 - self.q) // self.Q
+        pl.semaphore_wait(barrier, count)
+
+
+class ShardGather:
+    @staticmethod
+    def scratch(F):
+        n = 6 if F == 4 else F - 1
+        return [pltpu.SemaphoreType.DMA((n,)), pltpu.SemaphoreType.DMA((n,)),
+                pltpu.SemaphoreType.DMA]
+
+    def __init__(self, at, src, dst, send, recv, local):
+        self.at, self.src, self.dst = at, src, dst
+        f, j = at.f, at.j
+        self.own = pltpu.make_async_copy(src, dst.at[f], local)
+        self.first, self.later, self.arrivals = [], [], []
+        if at.F == 4:
+            nx = f + 1 - 2 * lax.rem(f, 2)
+            ny = lax.rem(f + 2, 4)
+            nd = lax.rem(nx + 2, 4)
+            half = src.shape[0] // 2
+            a, b = pl.ds(0, half), pl.ds(half, half)
+            table = ((nx, a), (nx, b), (ny, a), (ny, b))
+            for i, (to, rows) in enumerate(table):
+                self.first.append(
+                    remote(src.at[rows], dst.at[f, rows], send.at[i], recv.at[i], (j, to))
+                )
+                self.arrivals.append(
+                    remote(src.at[rows], dst.at[to, rows], send.at[i], recv.at[i], (j, to))
+                )
+            for i, (of, rows, to) in ((4, (nx, a, ny)), (5, (ny, b, nx))):
+                self.later.append(
+                    remote(dst.at[of, rows], dst.at[of, rows], send.at[i], recv.at[i], (j, to))
+                )
+                self.arrivals.append(
+                    remote(dst.at[nd, rows], dst.at[nd, rows], send.at[i], recv.at[i], (j, to))
+                )
+        else:
+            for k in range(1, at.F):
+                to, of = lax.rem(f + k, at.F), lax.rem(f + at.F - k, at.F)
+                self.first.append(
+                    remote(src, dst.at[f], send.at[k - 1], recv.at[k - 1], (j, to))
+                )
+                self.arrivals.append(
+                    remote(src, dst.at[of], send.at[k - 1], recv.at[k - 1], (j, to))
+                )
+
+    def start(self):
+        self.own.start()
+        for copy in self.first:
+            copy.start()
+
+    def relay(self):
+        if self.later:
+            self.arrivals[0].wait_recv()
+            self.later[0].start()
+            self.arrivals[3].wait_recv()
+            self.later[1].start()
+
+    def finish(self):
+        for i, copy in enumerate(self.arrivals):
+            if not (self.later and i in (0, 3)):
+                copy.wait_recv()
+        for copy in self.first + self.later:
+            copy.wait_send()
+        self.own.wait()
+
+
+class TokenGather:
+    @staticmethod
+    def scratch(S):
+        Q = S // 2
+        return [pltpu.SemaphoreType.DMA((2 * Q,)), pltpu.SemaphoreType.DMA((2 * Q,)),
+                pltpu.SemaphoreType.DMA((S,)), pltpu.SemaphoreType.DMA]
+
+    def __init__(self, at, src, dst, send, share, recv, local):
+        self.at, self.src, self.dst = at, src, dst
+        self.send, self.share, self.recv = send, share, recv
+        self.own = pltpu.make_async_copy(src, dst.at[at.j], local)
+
+    def onward(self, slot, source, i, by):
+        to = self.dst.at[slot]
+        return remote(
+            source, to, self.send.at[i], self.recv.at[slot], (self.at.j + by, self.at.f)
+        )
+
+    def given(self, slot, source, i):
+        to = self.dst.at[slot]
+        return remote(
+            source, to, self.share.at[i], self.recv.at[slot], (self.at.partner, self.at.f)
+        )
+
+    def plan(self, d):
+        at, Q = self.at, self.at.Q
+        below, above = at.j - 2 * d, at.j + 2 * d
+        dst = self.dst
+        return (
+            (at.q >= d, self.onward(below, dst.at[below], d, 2), at.q < Q - 1,
+             self.given(below, dst.at[below], d)),
+            (at.q + d <= Q - 1, self.onward(above, dst.at[above], Q + d, -2), at.q > 0,
+             self.given(above, dst.at[above], Q + d)),
+        )
+
+    def ends(self):
+        j, Q = self.at.j, self.at.Q
+        return (
+            self.onward(j, self.src, 0, 2), self.onward(j, self.src, Q, -2),
+            self.given(j, self.src, 0),
+        )
+
+    def start(self):
+        at, Q = self.at, self.at.Q
+        self.own.start()
+        up, down, part = self.ends()
+
+        @pl.when(at.q < Q - 1)
+        def _():
+            up.start()
+
+        @pl.when(at.q > 0)
+        def _():
+            down.start()
+
+        part.start()
+
+    def step(self, d):
+        for valid, onward, go, part in self.plan(d):
+
+            @pl.when(valid)
+            def _():
+                onward.wait_recv()
+
+                @pl.when(go)
+                def _():
+                    onward.start()
+
+                part.start()
+
+    def finish(self):
+        at, Q = self.at, self.at.Q
+        for q in range(Q):
+            slot = 2 * q + 1 - at.c
+            self.given(slot, self.dst.at[slot], 0).wait_recv()
+        up, down, part = self.ends()
+
+        @pl.when(at.q < Q - 1)
+        def _():
+            up.wait_send()
+
+        @pl.when(at.q > 0)
+        def _():
+            down.wait_send()
+
+        part.wait_send()
+        for d in range(1, Q):
+            for valid, onward, go, part in self.plan(d):
+
+                @pl.when(valid & go)
+                def _():
+                    onward.wait_send()
+
+                @pl.when(valid)
+                def _():
+                    part.wait_send()
+
+        self.own.wait()
+
+
+class GradReduce:
+    @staticmethod
+    def scratch(F, rows, n):
+        return [pltpu.VMEM((F, rows, n), BF), pltpu.VMEM((F - 1, rows, n), BF),
+                pltpu.SemaphoreType.DMA((F - 1,)), pltpu.SemaphoreType.DMA((F - 1,))]
+
+    def __init__(self, at, left, right, extra, made, got, send, recv):
+        self.at, self.left, self.right, self.extra = at, left, right, extra
+        self.made, self.got, self.send, self.recv = made, got, send, recv
+        self.n = right.shape[1]
+        self.rows = left.shape[1] // at.F
+        self.tile = 512 if self.n % 512 == 0 else 256 if self.n % 256 == 0 else 128
+
+    def copy(self, k):
+        at = self.at
+        to = lax.rem(at.f + k, at.F)
+        return remote(
+            self.made.at[to], self.got.at[k - 1], self.send.at[k - 1], self.recv.at[k - 1],
+            (at.j, to),
+        )
+
+    def start(self):
+        at, rows = self.at, self.rows
+        aligned = rows % 128 == 0
+        for t in range(0, self.n, self.tile) if not aligned else ():
+            cols = slice(t, t + self.tile)
+            full = dot_tn(self.left[...], self.right[:, cols]).astype(BF)
+            for p in range(at.F):
+                self.made[p, 0:rows, cols] = full[p * rows : (p + 1) * rows, :]
+        for k in list(range(1, at.F)) + [0]:
+            p = lax.rem(at.f + k, at.F)
+            if aligned:
+                block = self.left[:, pl.ds(pl.multiple_of(p * rows, 128), rows)]
+                for t in range(0, self.n, self.tile):
+                    cols = slice(t, t + self.tile)
+                    self.made[p, 0:rows, cols] = dot_tn(block, self.right[:, cols]).astype(BF)
+            if self.extra is not None:
+                self.made[p, rows : rows + self.extra.shape[1], :] = self.extra[p].astype(BF)
+            if k:
+                self.copy(k).start()
+
+    def finish(self, store):
+        at = self.at
+        for k in range(1, at.F):
+            self.copy(k).wait_recv()
+        for t in range(0, self.n, self.tile):
+            cols = slice(t, t + self.tile)
+            total = self.made[at.f, :, cols].astype(F32)
+            for k in range(1, at.F):
+                total += self.got[k - 1, :, cols].astype(F32)
+            store(t, self.tile, total.astype(BF))
+        for k in range(1, at.F):
+            self.copy(k).wait_send()
+
+
+EXTRA = 16
+
+
+def exchange(S, F, collective_id, grads=(), shards=(), tokens=(), merge=None):
+    operands, in_specs = [], []
+    vmem = pl.BlockSpec(memory_space=pltpu.VMEM)
+    outs, out_specs, scratch = [], [], []
+    shapes, row = [], 0
+    for left, right, extra in grads:
+        rows, n = left.shape[1] // F + (0 if extra is None else EXTRA), right.shape[1]
+        operands += [left, right] + ([] if extra is None else [extra])
+        scratch += GradReduce.scratch(F, rows, n)
+        shapes.append((rows, n, row))
+        row += rows * pl.cdiv(n, merge or n)
+        if not merge:
+            outs.append(jax.ShapeDtypeStruct((rows, n), BF))
+    if merge:
+        outs.append(jax.ShapeDtypeStruct((row, merge), BF))
+    out_specs += [vmem] * len(outs)
+    for array in shards:
+        operands.append(array)
+        outs.append(jax.ShapeDtypeStruct((F,) + array.shape, BF))
+        out_specs.append(pl.BlockSpec(memory_space=pl.ANY))
+        scratch += ShardGather.scratch(F)
+    for array in tokens:
+        operands.append(array)
+        outs.append(jax.ShapeDtypeStruct((S,) + array.shape, BF))
+        out_specs.append(pl.BlockSpec(memory_space=pl.ANY))
+        scratch += TokenGather.scratch(S)
+    in_specs = [vmem] * len(operands)
+    n_in, n_out = len(operands), len(outs)
+
+    def kernel(*refs):
+        ins, results, rest = list(refs[:n_in]), list(refs[n_in : n_in + n_out]), list(
+            refs[n_in + n_out :]
+        )
+        take = lambda items, n: [items.pop(0) for _ in range(n)]
+        at = Place(S, F)
+        jobs, stores = [], []
+        packed = take(results, 1)[0] if merge else None
+        for (_, _, extra), (rows, n, row0) in zip(grads, shapes):
+            left, right = take(ins, 2)
+            extra_ref = None if extra is None else take(ins, 1)[0]
+            jobs.append(GradReduce(at, left, right, extra_ref, *take(rest, 4)))
+            target = packed if merge else take(results, 1)[0]
+
+            def store(t, width, value, target=target, rows=rows, row0=row0):
+                if not merge:
+                    target[:, t : t + width] = value
+                    return
+                while width:
+                    chunk, col = divmod(t, merge)
+                    part = min(width, merge - col)
+                    target[row0 + chunk * rows : row0 + (chunk + 1) * rows, col : col + part] = (
+                        value[:, :part]
+                    )
+                    value, t, width = value[:, part:], t + part, width - part
+
+            stores.append(store)
+        spreads = [
+            ShardGather(at, take(ins, 1)[0], take(results, 1)[0], *take(rest, 3)) for _ in shards
+        ]
+        lines = [
+            TokenGather(at, take(ins, 1)[0], take(results, 1)[0], *take(rest, 4)) for _ in tokens
+        ]
+        at.greet(bool(jobs or spreads), bool(lines))
+        for item in lines + spreads:
+            item.start()
+        for job in jobs:
+            job.start()
+        waiting = list(spreads)
+        for d in range(1, at.Q) if lines else ():
+            for item in lines:
+                item.step(d)
+            if waiting:
+                waiting.pop(0).relay()
+        for item in waiting:
+            item.relay()
+        for job, store in zip(jobs, stores):
+            job.finish(store)
+        for item in spreads + lines:
+            item.finish()
+
+    flops = sum(2 * l.shape[0] * l.shape[1] * r.shape[1] for l, r, _ in grads)
+    moved = sum(o.size * 2 for o in outs)
+    return pl.pallas_call(
+        kernel,
+        out_shape=tuple(outs),
+        in_specs=in_specs,
+        out_specs=tuple(out_specs),
+        scratch_shapes=scratch,
+        compiler_params=pltpu.CompilerParams(
+            collective_id=collective_id, has_side_effects=True
+        ),
+        cost_estimate=pl.CostEstimate(
+            flops=flops, bytes_accessed=20 * moved, transcendentals=0
+        ),
+    )(*operands)
+
+
+def seq_sum(S, F, collective_id, arrays):
+    Q = S // 2
+    t, d = arrays[0].shape[1:]
+    n = len(arrays)
+
+    def kernel(*refs):
+        at = Place(S, F)
+        jobs = []
+        for i in range(n):
+            scratch = refs[2 * n + 7 * i : 2 * n + 7 * (i + 1)]
+            jobs.append((refs[i], refs[n + i]) + tuple(scratch))
+        at.greet(False, True)
+
+        def share(job, q):
+            part, _, pair, _, _, _, _, s_pair, r_pair = job[:9]
+            return remote(
+                part.at[2 * q + 1 - at.c], pair.at[q], s_pair.at[q], r_pair.at[q],
+                (at.partner, at.f),
+            )
+
+        def hop(job, q, up):
+            _, _, _, buf, got, s_line, r_line, _, _ = job[:9]
+            i = q if up else Q + q
+            return remote(
+                buf.at[i], got.at[i], s_line.at[i], r_line.at[i],
+                (at.j + 2 if up else at.j - 2, at.f),
+            )
+
+        order = []
+        for i in range(Q):
+            for q in (Q - 1 - i, i):
+                if q not in order:
+                    order.append(q)
+        for q in order:
+            for job in jobs:
+                share(job, q).start()
+
+        def base(job, q):
+            share(job, q).wait_recv()
+            return job[0][2 * q + at.c].astype(F32) + job[2][q].astype(F32)
+
+        for i in range(Q - 1):
+            for job in jobs:
+                for q, up in ((Q - 1 - i, True), (i, False)):
+                    sends = at.q < q if up else at.q > q
+                    inner = at.q > 0 if up else at.q < Q - 1
+                    copy = hop(job, q, up)
+                    slot = q if up else Q + q
+
+                    @pl.when(sends)
+                    def _():
+                        value = base(job, q)
+                        job[3][slot] = value.astype(BF)
+
+                        @pl.when(inner)
+                        def _():
+                            copy.wait_recv()
+                            job[3][slot] = (value + job[4][slot].astype(F32)).astype(BF)
+
+                        copy.start()
+
+        for job in jobs:
+            for q in range(Q):
+
+                @pl.when(at.q == q)
+                def _():
+                    job[1][...] = base(job, q)
+                    if q > 0:
+                        hop(job, q, True).wait_recv()
+                        job[1][...] += job[4][q].astype(F32)
+                    if q < Q - 1:
+                        hop(job, q, False).wait_recv()
+                        job[1][...] += job[4][Q + q].astype(F32)
+
+        for job in jobs:
+            for q in range(Q):
+                share(job, q).wait_send()
+
+                @pl.when(at.q < q)
+                def _():
+                    hop(job, q, True).wait_send()
+
+                @pl.when(at.q > q)
+                def _():
+                    hop(job, q, False).wait_send()
+
+    vmem = pl.BlockSpec(memory_space=pltpu.VMEM)
+    scratch = [
+        pltpu.VMEM((Q, t, d), BF),
+        pltpu.VMEM((2 * Q, t, d), BF),
+        pltpu.VMEM((2 * Q, t, d), BF),
+        pltpu.SemaphoreType.DMA((2 * Q,)),
+        pltpu.SemaphoreType.DMA((2 * Q,)),
+        pltpu.SemaphoreType.DMA((Q,)),
+        pltpu.SemaphoreType.DMA((Q,)),
+    ]
+    return pl.pallas_call(
+        kernel,
+        out_shape=tuple(jax.ShapeDtypeStruct((t, d), F32) for _ in arrays),
+        in_specs=[vmem] * n,
+        out_specs=tuple([vmem] * n),
+        scratch_shapes=scratch * n,
+        compiler_params=pltpu.CompilerParams(
+            collective_id=collective_id, has_side_effects=True
+        ),
+        cost_estimate=pl.CostEstimate(
+            flops=n * S * t * d, bytes_accessed=40 * n * S * t * d, transcendentals=0
+        ),
+    )(*arrays)
+
+
+def half_lanes(first, second, odd):
+    lane = lax.broadcasted_iota(jnp.int32, first.shape, 1)
+    if odd:
+        first = pltpu.roll(first, HEAD, 1)
+    else:
+        second = pltpu.roll(second, HEAD, 1)
+    return jnp.where(lane < HEAD, first, second)
+
+
+def pick_qkv(weight, j, F, S, pairs):
+    rows = weight.shape[0]
+    per_shard = S // 2
+
+    def kernel(j_ref, first, second, out):
+        a, b = first[...].astype(F32), second[...].astype(F32)
+
+        @pl.when(j_ref[0] % 2 == 0)
+        def _():
+            out[...] = half_lanes(a, b, 0).astype(BF)
+
+        @pl.when(j_ref[0] % 2 == 1)
+        def _():
+            out[...] = half_lanes(a, b, 1).astype(BF)
+
+    def column(which):
+        return lambda i, j_ref: (
+            0, (i % 3) * F * per_shard + (2 * (i // 3) + which) * per_shard + j_ref[0] // 2
+        )
+
+    return pl.pallas_call(
+        kernel,
+        grid_spec=pltpu.PrefetchScalarGridSpec(
+            num_scalar_prefetch=1,
+            grid=(3 * pairs,),
+            in_specs=[pl.BlockSpec((rows, LANES), column(0)), pl.BlockSpec((rows, LANES), column(1))],
+            out_specs=pl.BlockSpec((rows, LANES), lambda i, j_ref: (0, i)),
+        ),
+        out_shape=jax.ShapeDtypeStruct((rows, 3 * pairs * LANES), BF),
+    )(j[None].astype(jnp.int32), weight, weight)
+
+
+def unpack_qkv(gathered, rows, S, pairs):
+    width = S * HEAD
+
+    def kernel(src, out):
+        for half in range(2):
+            for z in range(S // 2):
+                a, b = src[2 * z].astype(F32), src[2 * z + 1].astype(F32)
+                out[:, half * width + z * LANES : half * width + (z + 1) * LANES] = half_lanes(
+                    a, b, half
+                )
+
+    return pl.pallas_call(
+        kernel,
+        grid=(3 * pairs,),
+        in_specs=[pl.BlockSpec((S, rows, LANES), lambda i: (0, 0, i))],
+        out_specs=pl.BlockSpec((rows, 2 * width), lambda i: (0, (i % 3) * pairs + i // 3)),
+        out_shape=jax.ShapeDtypeStruct((rows, HEADS * HEAD * 3), F32),
+    )(gathered)
+
+
+def unpack_cols(gathered, rows, F):
+    S, _, cols = gathered.shape
+    w = cols // F
+    if w % LANES:
+        split = gathered[:, :rows].reshape(S, rows, F, w)
+        return split.transpose(1, 2, 0, 3).reshape(rows, F * S * w).astype(F32)
+
+    def kernel(src, out):
+        for s in range(S):
+            out[:, s * w : (s + 1) * w] = src[s].astype(F32)
+
+    return pl.pallas_call(
+        kernel,
+        grid=(F,),
+        in_specs=[pl.BlockSpec((S, rows, w), lambda i: (0, 0, i))],
+        out_specs=pl.BlockSpec((rows, S * w), lambda i: (0, i)),
+        out_shape=jax.ShapeDtypeStruct((rows, F * S * w), F32),
+    )(gathered)
+
+
+def unpack_rows(gathered, rows):
+    S, _, n = gathered.shape
+
+    def kernel(src, out):
+        out[...] = src[0].astype(F32)
+
+    return pl.pallas_call(
+        kernel,
+        grid=(S,),
+        in_specs=[pl.BlockSpec((1, rows, n), lambda i: (i, 0, 0))],
+        out_specs=pl.BlockSpec((rows, n), lambda i: (i, 0)),
+        out_shape=jax.ShapeDtypeStruct((S * rows, n), F32),
+    )(gathered)
+
+
 def body(
     tokens,
     ln_gain,
@@ -180,6 +755,8 @@
     spread = per_shard % S == 0
     slots = per_shard // S if spread else 0
 
+    qkv_width = pairs * 3 * LANES
+
     def heads_of(array, lead):
         shape = array.shape
         if spread:
@@ -193,6 +770,16 @@
         mine = heads_of(array.reshape(n, 3, HEADS, HEAD), 2)
         return mine.reshape(n, 3, pairs, 2, HEAD).transpose(0, 2, 1, 3, 4).reshape(n, -1)
 
+    def from_qkv_cols(gathered):
+        n = gathered.shape[1]
+        split = gathered.reshape(S, n, pairs, 3, 2, HEAD).transpose(0, 1, 3, 2, 4, 5)
+        split = split.reshape(S, n, 3, hp, HEAD)
+        if spread:
+            moved = jnp.moveaxis(split.reshape(S, n, 3, F, slots, HEAD), 0, 3)
+        else:
+            moved = jnp.moveaxis(split, 0, 2)
+        return moved.reshape(n, -1)
+
     small = jnp.concatenate([ln_gain, ln_bias, qkv_bias, dense_bias, fc1_bias, fc2_bias])
     small = lax.all_gather(small, "fsdp", axis=0)
     cuts, at = [], 0
@@ -208,113 +795,102 @@
     standard = (inputs - centre) * inv_std
     normed_own = (standard * gain + shift).astype(BF)
     upstream_own = cotangent[0]
-    normed = lax.all_gather(normed_own, "seq", axis=0, tiled=True)
-    upstream = lax.all_gather(upstream_own, "seq", axis=0, tiled=True)
 
     up_own = lax.dynamic_index_in_dim(
         fc1_weight.reshape(rows_d, F, S, block_up), j, 2, keepdims=False
     ).reshape(rows_d, cols_up)
-    w_up = lax.all_gather(up_own, "fsdp", axis=0, tiled=True)
     down_own = lax.dynamic_slice_in_dim(fc2_weight, j * block_up, block_up, 0)
-    w_down = lax.all_gather(down_own, "fsdp", axis=0, tiled=True)
-    w_qkv = lax.all_gather(qkv_cols(qkv_weight), "fsdp", axis=0, tiled=True)
+    if spread and slots == 1:
+        qkv_own = pick_qkv(qkv_weight, j, F, S, pairs)
+    else:
+        qkv_own = qkv_cols(qkv_weight)
+    w_up, w_down, normed, upstream = exchange(
+        S, F, 1, shards=(up_own, down_own), tokens=(normed_own, upstream_own)
+    )
+    w_up, w_down = w_up.reshape(D, cols_up), w_down.reshape(cols_up, D)
+    normed, upstream = normed.reshape(length, D), upstream.reshape(length, D)
+
+    bias_up = lax.dynamic_index_in_dim(b_up.reshape(F, S, block_up), j, 1, keepdims=False)
+    bias_up = bias_up.reshape(-1)
+    bias_qkv = qkv_cols(b_qkv[None])[0]
+    seg_row = segments[0]
+
+    def rider(values, width):
+        return jnp.pad(values[:, None], ((0, 0), (0, EXTRA - 1), (0, width - values.shape[1])))
+
+    pre_act = dot(normed, w_up) + bias_up
+    activated = gelu_tanh(pre_act).astype(BF)
+    out_term = jnp.sum(upstream.astype(F32), axis=0).reshape(F, rows_d)
+    (piece_down,) = exchange(S, F, 2, grads=((activated, upstream, rider(out_term, D)),))
+    piece_down, qkv_own = lax.optimization_barrier((piece_down, qkv_own))
+    out_mine = piece_down[block_up, :rows_d].astype(F32)
+    all_down = lax.all_gather(piece_down, "seq", axis=0)
+
+    grad_act = dot_nt(upstream, w_down)
+    grad_pre = jax.vjp(gelu_tanh, pre_act)[1](grad_act)[0].astype(BF)
+    up_term = jnp.sum(grad_pre.astype(F32), axis=0).reshape(F, block_up)
+    block_dense = slots * HEAD
+    shards = (qkv_own,)
     if spread:
-        block_dense = slots * HEAD
-        dense_own = lax.dynamic_slice_in_dim(dense_weight, j * block_dense, block_dense, 0)
-        w_dense = lax.all_gather(dense_own, "fsdp", axis=0, tiled=True)
+        shards += (lax.dynamic_slice_in_dim(dense_weight, j * block_dense, block_dense, 0),)
+    piece_up, w_qkv, *w_dense = exchange(
+        S, F, 3, grads=((normed, grad_pre, rider(up_term, cols_up)),), shards=shards
+    )
+    all_up = lax.all_gather(piece_up, "seq", axis=0)
+    w_qkv = w_qkv.reshape(D, qkv_width)
+    if spread:
+        w_dense = w_dense[0].reshape(hp * HEAD, D)
     else:
         w_dense = lax.dynamic_slice_in_dim(
             lax.all_gather(dense_weight, "fsdp", axis=0, tiled=True), j * hp * HEAD, hp * HEAD, 0
         )
 
-    bias_up = lax.dynamic_index_in_dim(b_up.reshape(F, S, block_up), j, 1, keepdims=False)
-    bias_up = bias_up.reshape(-1)
-    bias_qkv = qkv_cols(b_qkv[None])[0]
-    seg_row = segments[0]
-
-    pre_act = dot(normed, w_up) + bias_up
-    activated = gelu_tanh(pre_act).astype(BF)
-    grad_act = dot_nt(upstream, w_down)
-    grad_pre = jax.vjp(gelu_tanh, pre_act)[1](grad_act)[0].astype(BF)
     projected = dot(normed, w_qkv) + bias_qkv
     grad_att = dot_nt(upstream, w_dense).astype(BF)
     attended, grad_mixed = attention(projected, grad_att, angle_tables(seg_row), seg_row)
-
-    partial_out = dot(attended, w_dense) + dot(activated, w_down)
-    branches = lax.psum_scatter(partial_out.astype(BF), "seq", scatter_dimension=0, tiled=True)
-    result = (inputs + branches.astype(F32) + (b_dense + b_down)).astype(BF)
-
-    partial_normed = dot_nt(grad_mixed, w_qkv) + dot_nt(grad_pre, w_up)
-    grad_normed = lax.psum_scatter(
-        partial_normed.astype(BF), "seq", scatter_dimension=0, tiled=True
-    ).astype(F32)
+    qkv_term = jnp.sum(grad_mixed.astype(F32), axis=0)
+    qkv_term = jnp.broadcast_to(qkv_term[None], (F, qkv_width))
+    grads = ((normed, grad_mixed, rider(qkv_term, qkv_width)),)
+    if spread:
+        grads += ((attended, upstream, None),)
+    (piece_qkv,) = exchange(S, F, 4, grads=grads, merge=qkv_width)
+    all_qkv = lax.all_gather(piece_qkv, "seq", axis=0)
+
+    partial_out = (dot(attended, w_dense) + dot(activated, w_down)).astype(BF)
+    partial_normed = (dot_nt(grad_mixed, w_qkv) + dot_nt(grad_pre, w_up)).astype(BF)
+    branches, grad_normed = seq_sum(
+        S, F, 5, (partial_out.reshape(S, tok, D), partial_normed.reshape(S, tok, D))
+    )
+    result = (inputs + branches + (b_dense + b_down)).astype(BF)
     scaled = grad_normed * gain
     grad_inputs = upstream_own.astype(F32) + inv_std * (
         scaled
         - jnp.mean(scaled, axis=-1, keepdims=True)
         - standard * jnp.mean(scaled * standard, axis=-1, keepdims=True)
     )
-
-    def summed(left, right):
-        return lax.psum_scatter(
-            dot_tn(left, right).astype(BF), "fsdp", scatter_dimension=0, tiled=True
-        )
-
-    piece_down = summed(activated, upstream)
-    piece_up = summed(normed, grad_pre)
-    piece_qkv = summed(normed, grad_mixed)
-    grad_down = lax.all_gather(piece_down, "seq", axis=0, tiled=True).astype(F32)
-    grad_up = (
-        lax.all_gather(piece_up, "seq", axis=0)
-        .reshape(S, rows_d, F, block_up)
-        .transpose(1, 2, 0, 3)
-        .reshape(rows_d, ff)
-        .astype(F32)
-    )
-
-    def to_heads(array, lead):
-        shape = array.shape
-        if spread:
-            split = array.reshape(shape[: 1 + lead] + (F, slots) + shape[2 + lead :])
-            moved = jnp.moveaxis(split, 0, lead + 1)
-        else:
-            moved = jnp.moveaxis(array, 0, lead)
-        return moved.reshape(shape[1 : 1 + lead] + (HEADS,) + shape[2 + lead :])
-
-    def from_qkv_cols(gathered):
-        n = gathered.shape[1]
-        split = gathered.reshape(S, n, pairs, 3, 2, HEAD).transpose(0, 1, 3, 2, 4, 5)
-        return to_heads(split.reshape(S, n, 3, hp, HEAD), 2).reshape(n, -1)
-
-    grad_qkv = from_qkv_cols(lax.all_gather(piece_qkv, "seq", axis=0)).astype(F32)
+    ln_terms = jnp.stack([jnp.sum(grad_normed * standard, axis=0), jnp.sum(grad_normed, axis=0)])
+    ln_terms = lax.psum(ln_terms, ("seq", "fsdp"))
+    ln_mine = lax.dynamic_slice_in_dim(ln_terms, f * rows_d, rows_d, 1)
+
+    grad_down = unpack_rows(all_down, block_up)
+    grad_up = unpack_cols(all_up, rows_d, F)
+    up_mine = all_up[:, rows_d, :block_up].astype(F32).reshape(-1)
+    qkv_sums = from_qkv_cols(all_qkv[:, rows_d][:, None]).reshape(F, -1)
+    qkv_mine = lax.dynamic_index_in_dim(qkv_sums, f, 0, keepdims=False).astype(F32)
+    if spread and slots == 1:
+        grad_qkv = unpack_qkv(all_qkv, rows_d, S, pairs)
+    else:
+        grad_qkv = from_qkv_cols(all_qkv[:, :rows_d]).astype(F32)
     if spread:
-        piece_dense = summed(attended, upstream)
-        grad_dense = lax.all_gather(piece_dense, "seq", axis=0, tiled=True).astype(F32)
+        chunks, at = [], rows_d + EXTRA
+        for col in range(0, D, qkv_width):
+            n = min(qkv_width, D - col)
+            chunks.append(all_qkv[:, at : at + block_dense, :n])
+            at += block_dense
+        grad_dense = jnp.concatenate(chunks, axis=2).astype(F32).reshape(rows_d, D)
     else:
         part = lax.all_gather(dot_tn(attended, upstream).astype(BF), "seq", axis=0, tiled=True)
         grad_dense = lax.psum_scatter(part, "fsdp", scatter_dimension=0, tiled=True).astype(F32)
-
-    ln_terms = jnp.concatenate(
-        [jnp.sum(grad_normed * standard, axis=0), jnp.sum(grad_normed, axis=0)]
-    )
-    ln_terms = lax.psum_scatter(ln_terms, "seq", scatter_dimension=0, tiled=True)
-    out_term = jnp.sum(upstream.astype(F32), axis=0)
-    out_term = lax.dynamic_slice_in_dim(out_term, j * (D // S), D // S, 0)
-    up_term = jnp.sum(grad_pre.astype(F32), axis=0)
-    qkv_term = jnp.sum(grad_mixed.astype(F32), axis=0)
-    terms = lax.psum(jnp.concatenate([ln_terms, out_term, up_term, qkv_term]), "fsdp")
-    terms = lax.all_gather(terms, "seq", axis=0)
-    n_ln = 2 * D // S
-    n_out = n_ln + D // S
-    n_up = n_out + cols_up
-    ln_full = terms[:, :n_ln].reshape(2, F, rows_d)
-    ln_mine = lax.dynamic_index_in_dim(ln_full, f, 1, keepdims=False)
-    out_full = terms[:, n_ln:n_out].reshape(F, rows_d)
-    out_mine = lax.dynamic_index_in_dim(out_full, f, 0, keepdims=False)
-    up_full = terms[:, n_out:n_up].reshape(S, F, block_up)
-    up_mine = lax.dynamic_index_in_dim(up_full, f, 1, keepdims=False).reshape(-1)
-    qkv_full = from_qkv_cols(terms[:, n_up:][:, None]).reshape(F, -1)
-    qkv_mine = lax.dynamic_index_in_dim(qkv_full, f, 0, keepdims=False)
     return (
         result[None],
         grad_inputs[None],

time: 872 us -> 693 us (0.79)
  waiting for transfers between devices: 477 us -> 0.72 us
  Pallas kernels: 21.5 us -> 461 us
  local copies, waits for them, and re-layouts: 166 us -> 45.9 us
  matrix products: 87.2 us -> 45.2 us
  blocking collectives: 67.1 us -> 94.2 us
    pallas_call x0 -> x9, Pallas kernels: none -> 440 us  [the longest x4 276 us: exchange(): pl.pallas_call(kernel, out_shape=tuple(outs), in_specs=in_specs, out_spec...]
    all_gather x10 -> x3, waiting for transfers between devices: 294 us -> 0.01 us  [the longest x1 0.01 us: body(): all_up = lax.all_gather(piece_up, 'seq', axis=0)]
    reduce_scatter x6 -> x0, waiting for transfers between devices: 182 us -> none  [the longest x4 135 us: summed(): lax.psum_scatter(dot_tn(left, right).astype(BF), 'fsdp', scatter_dimensio...]
    convert_element_type x5 -> x0, local copies, waits for them, and re-layouts: 70.9 us -> none  [the longest x3 38.7 us: body(): from_qkv_cols(lax.all_gather(piece_qkv, 'seq', axis=0)).astype(F32)]
    psum x1, blocking collectives: 16 us -> 84.4 us  [body(): ln_terms = lax.psum(ln_terms, ('seq', 'fsdp'))]
    unnamed x62 -> x50, local copies, waits for them, and re-layouts: 79.2 us -> 17.8 us
    dot_general x4 -> x0, matrix products: 29.3 us -> none  [dot_tn(): lax.dot_general(left, right, (((0,), (0,)), ((), ())), preferred_element_...]
    unnamed x1 -> x0, blocking collectives: 27.3 us -> none
  transfers between devices with their start and end apart: 16 -> 3, of which waited for: 14 -> 0; matrix products, arithmetic and copies ran while one was open for 31% -> 8% of each run, Pallas kernels for 2% -> 33%
where the time goes in v2:
time: 693 us; the launch traced here: 682 us
  Pallas kernels  461 us (67%)
  blocking collectives  94.2 us (14%)
  local copies, waits for them, and re-layouts  45.9 us (7%)
  matrix products  45.2 us (7%)
  other arithmetic  20.6 us (3%)
  between operations  14.6 us (2%)
    pallas_call x4, Pallas kernels, exchange(): pl.pallas_call(kernel, out_shape=tuple(outs), in_specs=in_specs, out_spec...  276 us
    pallas_call x1, Pallas kernels, seq_sum(): pl.pallas_call(kernel, out_shape=tuple((jax.ShapeDtypeStruct((t, d), F32)...  129 us
    psum x1, blocking collectives, body(): ln_terms = lax.psum(ln_terms, ('seq', 'fsdp'))  84.4 us
    dot_general x4, matrix products, dot_nt(): lax.dot_general(left, right, (((1,), (1,)), ((), ())), preferred_element_...  22.9 us
    dot_general x4, matrix products, dot(): lax.dot_general(left, right, (((1,), (0,)), ((), ())), preferred_element_...  22.2 us
    pallas_call x1, Pallas kernels, attention(): pl.pallas_call(functools.partial(attention_kernel, rows), grid=(pairs,),...  20.9 us
    unnamed x50, local copies, waits for them, and re-layouts  17.8 us
  transfers between devices with their start and end apart: 3, of which 0 were waited for; matrix products, arithmetic and copies ran while one was open for 8% of the time, Pallas kernels for 33%

profile of v2, /device:TPU:0, one launch (start us, length us, event | category | flops | bytes accessed | tf_op | source)
XLA Modules:
  0.0 681.7 jit_solution(2154557218507990386)
XLA Ops:
  12.2 9.8 %all-gather.4 = bf16[4,1,5632]{2,1,0:T(2,128)(2,1)S(1)} all-gather(bf16[1,1,5632]{2,1,0:T(2,128)(2,1)S(1)} %reshape.185), channel_id=2, replica_groups=mesh['seq'=8,'fsdp'=4] {'fsdp'}, dimensions={0}, use_global_device_ids=true | all-gather | bytes 56320 | tf_op jit(solution)/shard_map/all_gather | solution.py:784
  24.7 9.7 %copy.42 = bf16[64,8,32,256]{3,2,1,0:T(8,128)(2,1)} copy(bf16[64,8,32,256]{3,1,2,0:T(8,128)(2,1)} %bitcast.133) | data formatting | bytes 16777216
  34.4 10.9 %dynamic-slice_reduce_fusion = bf16[512,4,256]{2,1,0:T(4,128)(2,1)} fusion(bf16[512,4,8,256]{3,2,1,0:T(8,128)(2,1)} %bitcast.129, s32[]{:T(128)S(6)} %select_n.32), kind=kLoop, calls=%fused_computation.16 | loop fusion | bytes 2097156 | tf_op jit(solution)/shard_map/jit(dynamic_index_in_dim)/dynamic_slice | solution.py:799
  45.4 2.4 copy.43
  47.8 2.3 constant_dynamic-slice_fusion.4.refs_1_
  51.3 74.8 %shard_map.220 = (bf16[4,512,1024]{2,1,0:T(8,128)(2,1)}, bf16[4,256,2048]{2,1,0:T(8,128)(2,1)}, bf16[8,128,2048]{2,1,0:T(8,128)(2,1)}, bf16[8,128,2048]{2,1,0:T(8,128)(2,1)}) custom-call(bf16[512,1024]{1,0:T(8,128)(2,1)} %bitcast.134, bf16[256,2048]{1,0:T(8,128)(2,1)} %constant_dynamic-slice_fusion.4.refs_1_, bf16[128,2048]{1,0:T(8,128)(2,1)} %fusion.16.refs_2_, ...), custom_call_target="tpu_custom_call" | custom-call | bytes 335544320 | tf_op jit(solution)/shard_map/pallas_call | solution.py:506
  126.1 3.0 convert_reduce_fusion
  130.0 6.5 fusion.30
  136.5 8.8 %convert_reduce_fusion.1 = (f32[1024]{0:T(1024)S(1)}, bf16[1024,1024]{1,0:T(8,128)(2,1)}, bf16[1024,1024]{1,0:T(8,128)(2,1)}) fusion(f32[1024,1024]{1,0:T(8,128)S(1)} %fusion.30, f32[1024]{0:T(1024)S(1)} %bitcast.170, bf16[1024,2048]{1,0:T(8,128)(2,1)S(1)} %bitcast.138, bf16[1024,2048]{1,0:T(8,128)(2,1)S(1)} %bitcast.176), kind=kOutput, calls=%fused_computation.13 | convolution fusion | flops 4321180672 | bytes 16785408 | tf_op jit(solution)/shard_map/dot_general | solution.py:26
  146.0 5.1 shard_map.222.refs_3_
  151.1 57.5 %shard_map.221 = bf16[272,2048]{1,0:T(8,128)(2,1)} custom-call(bf16[1024,1024]{1,0:T(8,128)(2,1)} %get-tuple-element.46.refs_0_, bf16[1024,2048]{1,0:T(8,128)(2,1)} %bitcast.135, f32[4,16,2048]{2,1,0:T(8,128)} %pad.13.refs_2_), custom_call_target="tpu_custom_call" | custom-call | flops 4294967296 | bytes 22282240 | tf_op jit(solution)/shard_map/pallas_call | solution.py:506
  209.4 88.1 %shard_map.223 = (bf16[528,1024]{1,0:T(8,128)(2,1)}, bf16[4,512,768]{2,1,0:T(8,128)(2,1)}, bf16[4,64,2048]{2,1,0:T(8,128)(2,1)}) custom-call(bf16[1024,2048]{1,0:T(8,128)(2,1)} %bitcast.178, bf16[1024,1024]{1,0:T(8,128)(2,1)} %get-tuple-element.43.refs_1_, f32[4,16,1024]{2,1,0:T(8,128)} %pad.12.refs_2_, bf16[512,768]{1,0:T(8,128)(2,1)} %shard_map.222.refs_3_, ...), custom_call_target="tpu_custom_call" | custom-call | flops 4294967296 | bytes 105512960 | tf_op jit(solution)/shard_map/pallas_call | solution.py:506
  297.6 1.9 multiply_sine_fusion
  299.6 1.9 concatenate.25.sin_high
  301.5 1.7 concatenate.24.sin_low
  304.6 1.7 concatenate.23.cos
  306.4 4.5 convolution_convert_fusion.grad_out
  310.9 5.1 convolution_add_fusion.proj
  316.0 20.9 %shard_map.224 = (bf16[1024,256]{1,0:T(8,128)(2,1)}, bf16[1024,768]{1,0:T(8,128)(2,1)}) custom-call(f32[1024,768]{1,0:T(8,128)} %convolution_add_fusion.proj, bf16[1024,256]{1,0:T(8,128)(2,1)} %convolution_convert_fusion.grad_out, f32[1024,128]{1,0:T(8,128)} %concatenate.23.cos, f32[1024,128]{1,0:T(8,128)} %concatenate.24.sin_low, ...), custom_call_target="tpu_custom_call" | custom-call | flops 3758096384 | bytes 6291456 | tf_op jit(solution)/shard_map/pallas_call | solution.py:108
  339.3 55.8 %shard_map.226 = bf16[720,768]{1,0:T(8,128)(2,1)} custom-call(bf16[1024,2048]{1,0:T(8,128)(2,1)} %bitcast.179, bf16[1024,768]{1,0:T(8,128)(2,1)} %get-tuple-element.33.refs_1_, f32[4,16,768]{2,1,0:T(8,128)} %pad.14.refs_2_, bf16[1024,256]{1,0:T(8,128)(2,1)} %get-tuple-element.32.refs_3_, bf16[1024,2048]{1,0:T(8,128)(2,1)} %bitcast.137), custom_call_target="tpu_custom_call" | custom-call | flops 4294967296 | bytes 22118400 | tf_op jit(solution)/shard_map/pallas_call | solution.py:506
  396.5 7.2 %fusion.31 = f32[1024,2048]{1,0:T(8,128)S(1)} fusion(bf16[1024,1024]{1,0:T(8,128)(2,1)} %get-tuple-element.46.refs_0_, bf16[1024,2048]{1,0:T(8,128)(2,1)} %bitcast.175), kind=kOutput, calls=%fused_computation.73 | convolution fusion | flops 4294967296 | bytes 14680064 | tf_op jit(solution)/shard_map/dot_general | solution.py:22
  403.8 3.4 add_convert_fusion.1
  407.9 3.4 fusion.32
  411.4 6.1 add_convert_fusion
  417.5 129.0 %shard_map.225 = (f32[128,2048]{1,0:T(8,128)}, f32[128,2048]{1,0:T(8,128)}) custom-call(bf16[8,128,2048]{2,1,0:T(8,128)(2,1)} %bitcast.124, bf16[8,128,2048]{2,1,0:T(8,128)(2,1)} %bitcast.139), custom_call_target="tpu_custom_call" | custom-call | flops 4194304 | bytes 167772160 | tf_op jit(solution)/shard_map/pallas_call | solution.py:617
  546.6 1.7 fusion.22
  548.3 84.4 %psum.7 = f32[2,2048]{1,0:T(2,128)S(1)} all-reduce(f32[2,2048]{1,0:T(2,128)S(1)} %pad_maximum_fusion), channel_id=1, replica_groups=mesh['seq'=8,'fsdp'=4] {'seq','fsdp'}, use_global_device_ids=true, to_apply=%region_8.9 | all-reduce | flops 4096 | bytes 32768 | tf_op jit(solution)/shard_map/psum | solution.py:872
  633.3 3.3 fusion.21
  636.6 9.7 %shard_map.228 = f32[512,8192]{1,0:T(8,128)} custom-call(bf16[8,528,1024]{2,1,0:T(8,128)(2,1)} %bitcast.131), custom_call_target="tpu_custom_call" | custom-call | tf_op jit(solution)/shard_map/pallas_call | solution.py:704
  648.8 9.1 %shard_map.227 = f32[512,6144]{1,0:T(8,128)} custom-call(bf16[8,720,768]{2,1,0:T(8,128)(2,1)} %bitcast.126), custom_call_target="tpu_custom_call" | custom-call | tf_op jit(solution)/shard_map/pallas_call | solution.py:684
  661.2 2.6 maximum_convert_fusion
  663.8 10.4 %shard_map.229 = f32[2048,2048]{1,0:T(8,128)} custom-call(bf16[8,272,2048]{2,1,0:T(8,128)(2,1)} %bitcast.130), custom_call_target="tpu_custom_call" | custom-call | tf_op jit(solution)/shard_map/pallas_call | solution.py:719
  (98 shorter events, 24.1 us)
Async XLA Ops:
  7.2 201.5 %copy-start = (bf16[512,2048]{1,0:T(8,128)(2,1)S(1)}, bf16[512,2048]{1,0:T(8,128)(2,1)}, u32[]{:S(2)}) copy-start(bf16[512,2048]{1,0:T(8,128)(2,1)} %param.19) | copy-start | bytes 6291460
  7.2 629.4 %all-gather.11.cloned.1.call-start = ((), (), s32[]{:S(2)}) async-start(), calls=%async_computation.1 | async-start | bytes 9732096 | tf_op jit(solution)/shard_map/all_gather | solution.py:839
  34.4 15.7 %copy-start.2 = (bf16[1,128,2048]{2,1,0:T(8,128)(2,1)S(1)}, bf16[1,128,2048]{2,1,0:T(8,128)(2,1)}, u32[]{:S(2)}) copy-start(bf16[1,128,2048]{2,1,0:T(8,128)(2,1)} %param.14) | copy-start | bytes 1572868
  126.1 3.8 copy-start.11
  130.0 6.5 copy-start.3
  130.0 6.5 copy-start.13
  209.4 88.2 %copy-start.9 = (s32[1,1024]{1,0:T(1,128)S(1)}, s32[1,1024]{1,0:T(1,128)}, u32[]{:S(2)}) copy-start(s32[1,1024]{1,0:T(1,128)} %seg_row.1) | copy-start | bytes 12292
  297.5 350.1 %all-gather.9.cloned.1.call-start = ((), (), s32[]{:S(2)}) async-start(), calls=%async_computation | async-start | bytes 9953280 | tf_op jit(solution)/shard_map/all_gather | solution.py:857
  303.3 3.1 copy-start.6
  306.3 4.6 copy-start.14
  306.3 4.6 copy-start.15
  395.1 268.7 %all-gather.13.cloned.1.call-start = ((), (), s32[]{:S(2)}) async-start(), calls=%async_computation.2 | async-start | bytes 10027008 | tf_op jit(solution)/shard_map/all_gather | solution.py:827
  396.5 277.6 %copy-start.10 = (f32[1,512]{1,0:T(1,128)}, f32[1,512]{1,0:T(1,128)S(1)}, u32[]{:S(2)}) copy-start(f32[1,512]{1,0:T(1,128)S(1)} %slice_convert_fusion.3) | copy-start | bytes 6148
  396.5 7.3 %copy-start.7 = (bf16[4,64,2048]{2,1,0:T(8,128)(2,1)S(1)}, bf16[4,64,2048]{2,1,0:T(8,128)(2,1)}, u32[]{:S(2)}) copy-start(bf16[4,64,2048]{2,1,0:T(8,128)(2,1)} %get-tuple-element.31) | copy-start | bytes 3145732
  396.5 7.3 %copy-start.8 = (bf16[1024,256]{1,0:T(8,128)(2,1)S(1)}, bf16[1024,256]{1,0:T(8,128)(2,1)}, u32[]{:S(2)}) copy-start(bf16[1024,256]{1,0:T(8,128)(2,1)} %get-tuple-element.32.refs_3_) | copy-start | bytes 1572868
  403.8 3.4 copy-start.5
  403.8 4.1 copy-start.16
  407.9 3.5 copy-start.12
  407.9 3.5 copy-start.17
  417.5 215.8 %copy-start.4 = (bf16[1,128,2048]{2,1,0:T(8,128)(2,1)S(1)}, bf16[1,128,2048]{2,1,0:T(8,128)(2,1)}, u32[]{:S(2)}) copy-start(bf16[1,128,2048]{2,1,0:T(8,128)(2,1)} %param.26) | copy-start | bytes 1572868
  663.8 11.0 %copy-start.1 = (bf16[512,2048]{1,0:T(8,128)(2,1)S(1)}, bf16[512,2048]{1,0:T(8,128)(2,1)}, u32[]{:S(2)}) copy-start(bf16[512,2048]{1,0:T(8,128)(2,1)} %param.19) | copy-start | bytes 6291460
Sparse Core Ops, SparseCore 0:
  297.7 83.3 all-gather.10
  395.2 132.8 all-gather.8
  529.7 96.7 all-gather.12

commit v3 on v2

--- a/solution.py
+++ b/solution.py
@@ -170,30 +170,29 @@
 
     def greet(self, over_fsdp, over_seq):
         barrier = pltpu.get_barrier_semaphore()
+
+        def signal(j, f):
+            pl.semaphore_signal(barrier, inc=1, device_id=(j, f), device_id_type=MESH)
+
         count = 0
         if over_fsdp:
             for k in range(1, self.F):
-                pl.semaphore_signal(
-                    barrier, inc=1, device_id=(self.j, lax.rem(self.f + k, self.F)),
-                    device_id_type=MESH,
-                )
-            count = self.F - 1
-        if over_seq:
-            pl.semaphore_signal(
-                barrier, inc=1, device_id=(self.partner, self.f), device_id_type=MESH
-            )
+                signal(self.j, lax.rem(self.f + k, self.F))
+            count += self.F - 1
+        if over_seq == "all":
+            for k in range(1, self.S):
+                signal(lax.rem(self.j + k, self.S), self.f)
+            count += self.S - 1
+        elif over_seq == "line":
+            signal(self.partner, self.f)
 
             @pl.when(self.q > 0)
             def _():
-                pl.semaphore_signal(
-                    barrier, inc=1, device_id=(self.j - 2, self.f), device_id_type=MESH
-                )
+                signal(self.j - 2, self.f)
 
             @pl.when(self.q < self.Q - 1)
             def _():
-                pl.semaphore_signal(
-                    barrier, inc=1, device_id=(self.j + 2, self.f), device_id_type=MESH
-                )
+                signal(self.j + 2, self.f)
 
             count += 1 + (self.q + self.Q - 1) // self.Q + (2 * self.Q - 2 - self.q) // self.Q
         pl.semaphore_wait(barrier, count)
@@ -421,7 +420,7 @@
 EXTRA = 16
 
 
-def exchange(S, F, collective_id, grads=(), shards=(), tokens=(), merge=None):
+def exchange(S, F, collective_id, grads=(), shards=(), tokens=(), merge=None, split=False):
     operands, in_specs = [], []
     vmem = pl.BlockSpec(memory_space=pltpu.VMEM)
     outs, out_specs, scratch = [], [], []
@@ -432,7 +431,10 @@
         scratch += GradReduce.scratch(F, rows, n)
         shapes.append((rows, n, row))
         row += rows * pl.cdiv(n, merge or n)
-        if not merge:
+        if split:
+            outs.append(jax.ShapeDtypeStruct((rows - EXTRA, n), BF))
+            outs.append(jax.ShapeDtypeStruct((EXTRA, n), BF))
+        elif not merge:
             outs.append(jax.ShapeDtypeStruct((rows, n), BF))
     if merge:
         outs.append(jax.ShapeDtypeStruct((row, merge), BF))
@@ -463,8 +465,13 @@
             extra_ref = None if extra is None else take(ins, 1)[0]
             jobs.append(GradReduce(at, left, right, extra_ref, *take(rest, 4)))
             target = packed if merge else take(results, 1)[0]
-
-            def store(t, width, value, target=target, rows=rows, row0=row0):
+            rider_ref = take(results, 1)[0] if split else None
+
+            def store(t, width, value, target=target, rows=rows, row0=row0, rider_ref=rider_ref):
+                if split:
+                    target[:, t : t + width] = value[: rows - EXTRA]
+                    rider_ref[:, t : t + width] = value[rows - EXTRA :]
+                    return
                 if not merge:
                     target[:, t : t + width] = value
                     return
@@ -483,7 +490,7 @@
         lines = [
             TokenGather(at, take(ins, 1)[0], take(results, 1)[0], *take(rest, 4)) for _ in tokens
         ]
-        at.greet(bool(jobs or spreads), bool(lines))
+        at.greet(bool(jobs or spreads), "line" if lines else "")
         for item in lines + spreads:
             item.start()
         for job in jobs:
@@ -518,115 +525,190 @@
     )(*operands)
 
 
-def seq_sum(S, F, collective_id, arrays):
+LN_ROWS = 8
+
+
+def token_sums(S, F, collective_id, out_part, normed_part, standard, pieces):
     Q = S // 2
-    t, d = arrays[0].shape[1:]
-    n = len(arrays)
+    t, d = out_part.shape[1:]
+    w = d // F
+    m = len(pieces)
+    n_in = 3 + m
 
     def kernel(*refs):
         at = Place(S, F)
-        jobs = []
-        for i in range(n):
-            scratch = refs[2 * n + 7 * i : 2 * n + 7 * (i + 1)]
-            jobs.append((refs[i], refs[n + i]) + tuple(scratch))
-        at.greet(False, True)
-
-        def share(job, q):
-            part, _, pair, _, _, _, _, s_pair, r_pair = job[:9]
+        ins, results, rest = refs[:n_in], refs[n_in : n_in + 3 + m], list(refs[n_in + 3 + m :])
+        take = lambda n: [rest.pop(0) for _ in range(n)]
+        jobs = [(ins[i], results[i]) + tuple(take(7)) for i in range(2)]
+        lines = [TokenGather(at, ins[3 + i], results[3 + i], *take(4)) for i in range(m)]
+        made, by_shard, by_seq, s_f, r_f, s_s, r_s = take(7)
+        j, f, q = at.j, at.f, at.q
+        low = 1 - q // (Q // 2)
+        at.greet(True, "all")
+
+        def share(job, slot):
+            part, _, pair, _, _, _, _, s_pair, r_pair = job
             return remote(
-                part.at[2 * q + 1 - at.c], pair.at[q], s_pair.at[q], r_pair.at[q],
-                (at.partner, at.f),
+                part.at[2 * slot + 1 - at.c], pair.at[slot], s_pair.at[slot], r_pair.at[slot],
+                (at.partner, f),
             )
 
-        def hop(job, q, up):
-            _, _, _, buf, got, s_line, r_line, _, _ = job[:9]
-            i = q if up else Q + q
+        def hop(job, slot, up):
+            _, _, _, buf, got, s_line, r_line, _, _ = job
+            i = slot + (1 - up) * Q
             return remote(
-                buf.at[i], got.at[i], s_line.at[i], r_line.at[i],
-                (at.j + 2 if up else at.j - 2, at.f),
+                buf.at[slot], got.at[i], s_line.at[i], r_line.at[i], (j + 4 * up - 2, f)
             )
 
         order = []
         for i in range(Q):
-            for q in (Q - 1 - i, i):
-                if q not in order:
-                    order.append(q)
-        for q in order:
+            for slot in (Q - 1 - i, i):
+                if slot not in order:
+                    order.append(slot)
+        for slot in order:
             for job in jobs:
-                share(job, q).start()
-
-        def base(job, q):
-            share(job, q).wait_recv()
-            return job[0][2 * q + at.c].astype(F32) + job[2][q].astype(F32)
-
+                share(job, slot).start()
+        for line in lines:
+            line.start()
+
+        def base(job, slot):
+            share(job, slot).wait_recv()
+            return job[0][2 * slot + at.c].astype(F32) + job[2][slot].astype(F32)
+
+        def pass_on(job, slot, up, inner):
+            copy = hop(job, slot, up)
+            i = slot + (1 - up) * Q
+
+            @pl.when((2 * up - 1) * (slot - q) > 0)
+            def _():
+                value = base(job, slot)
+                if inner is None:
+                    copy.wait_recv()
+                    job[3][slot] = (value + job[4][i].astype(F32)).astype(BF)
+                else:
+                    job[3][slot] = value.astype(BF)
+
+                    @pl.when(inner)
+                    def _():
+                        copy.wait_recv()
+                        job[3][slot] = (value + job[4][i].astype(F32)).astype(BF)
+
+                copy.start()
+
+        near = low * q + (1 - low) * (Q - 1 - q)
         for i in range(Q - 1):
             for job in jobs:
-                for q, up in ((Q - 1 - i, True), (i, False)):
-                    sends = at.q < q if up else at.q > q
-                    inner = at.q > 0 if up else at.q < Q - 1
-                    copy = hop(job, q, up)
-                    slot = q if up else Q + q
-
-                    @pl.when(sends)
-                    def _():
-                        value = base(job, q)
-                        job[3][slot] = value.astype(BF)
-
-                        @pl.when(inner)
-                        def _():
-                            copy.wait_recv()
-                            job[3][slot] = (value + job[4][slot].astype(F32)).astype(BF)
-
-                        copy.start()
+                pass_on(job, low * (Q - 1 - i) + (1 - low) * i, low, near > 0)
+            for job in jobs:
+                pass_on(job, (1 - low) * (Q - 1 - i) + low * i, 1 - low, None)
+            for line in lines:
+                line.step(i + 1)
 
         for job in jobs:
-            for q in range(Q):
-
-                @pl.when(at.q == q)
+            job[1][...] = base(job, q)
+
+            @pl.when(q > 0)
+            def _():
+                hop(job, q, 1).wait_recv()
+                job[1][...] += job[4][q].astype(F32)
+
+            @pl.when(q < Q - 1)
+            def _():
+                hop(job, q, 0).wait_recv()
+                job[1][...] += job[4][Q + q].astype(F32)
+
+        grad_normed = jobs[1][1][...]
+        gain_row = jnp.sum(grad_normed * ins[2][...], axis=0, keepdims=True)
+        bias_row = jnp.sum(grad_normed, axis=0, keepdims=True)
+        both = jnp.concatenate(
+            [gain_row, bias_row, jnp.zeros((LN_ROWS - 2, d), F32)], axis=0
+        )
+        for p in range(F):
+            made[p] = both[:, p * w : (p + 1) * w]
+        over_f = []
+        for k in range(1, F):
+            to, of = lax.rem(f + k, F), lax.rem(f + F - k, F)
+            over_f.append(
+                (remote(made.at[to], by_shard.at[f], s_f.at[k - 1], r_f.at[f], (j, to)),
+                 remote(made.at[to], by_shard.at[of], s_f.at[k - 1], r_f.at[of], (j, to)))
+            )
+        for copy, _ in over_f:
+            copy.start()
+        by_shard[f] = made[f]
+        for _, arrival in over_f:
+            arrival.wait_recv()
+        total = by_shard[0]
+        for p in range(1, F):
+            total += by_shard[p]
+        by_seq[j] = total
+        over_s = []
+        for k in range(1, S):
+            to, of = lax.rem(j + k, S), lax.rem(j + S - k, S)
+            over_s.append(
+                (remote(by_seq.at[j], by_seq.at[j], s_s.at[k - 1], r_s.at[j], (to, f)),
+                 remote(by_seq.at[j], by_seq.at[of], s_s.at[k - 1], r_s.at[of], (to, f)))
+            )
+        for copy, _ in over_s:
+            copy.start()
+        for _, arrival in over_s:
+            arrival.wait_recv()
+        total = by_seq[0]
+        for p in range(1, S):
+            total += by_seq[p]
+        results[2][...] = total
+        for copy, _ in over_f + over_s:
+            copy.wait_send()
+        for job in jobs:
+            for slot in range(Q):
+                share(job, slot).wait_send()
+
+                @pl.when(q < slot)
                 def _():
-                    job[1][...] = base(job, q)
-                    if q > 0:
-                        hop(job, q, True).wait_recv()
-                        job[1][...] += job[4][q].astype(F32)
-                    if q < Q - 1:
-                        hop(job, q, False).wait_recv()
-                        job[1][...] += job[4][Q + q].astype(F32)
-
-        for job in jobs:
-            for q in range(Q):
-                share(job, q).wait_send()
-
-                @pl.when(at.q < q)
+                    hop(job, slot, 1).wait_send()
+
+                @pl.when(q > slot)
                 def _():
-                    hop(job, q, True).wait_send()
-
-                @pl.when(at.q > q)
-                def _():
-                    hop(job, q, False).wait_send()
+                    hop(job, slot, 0).wait_send()
+
+        for line in lines:
+            line.finish()
 
     vmem = pl.BlockSpec(memory_space=pltpu.VMEM)
     scratch = [
         pltpu.VMEM((Q, t, d), BF),
-        pltpu.VMEM((2 * Q, t, d), BF),
+        pltpu.VMEM((Q, t, d), BF),
         pltpu.VMEM((2 * Q, t, d), BF),
         pltpu.SemaphoreType.DMA((2 * Q,)),
         pltpu.SemaphoreType.DMA((2 * Q,)),
         pltpu.SemaphoreType.DMA((Q,)),
         pltpu.SemaphoreType.DMA((Q,)),
+    ] * 2
+    for _ in pieces:
+        scratch += TokenGather.scratch(S)
+    scratch += [
+        pltpu.VMEM((F, LN_ROWS, w), F32),
+        pltpu.VMEM((F, LN_ROWS, w), F32),
+        pltpu.VMEM((S, LN_ROWS, w), F32),
+        pltpu.SemaphoreType.DMA((F - 1,)),
+        pltpu.SemaphoreType.DMA((F,)),
+        pltpu.SemaphoreType.DMA((S - 1,)),
+        pltpu.SemaphoreType.DMA((S,)),
     ]
+    full = jax.ShapeDtypeStruct((t, d), F32)
     return pl.pallas_call(
         kernel,
-        out_shape=tuple(jax.ShapeDtypeStruct((t, d), F32) for _ in arrays),
-        in_specs=[vmem] * n,
-        out_specs=tuple([vmem] * n),
-        scratch_shapes=scratch * n,
+        out_shape=(full, full, jax.ShapeDtypeStruct((LN_ROWS, w), F32))
+        + tuple(jax.ShapeDtypeStruct((S,) + p.shape, BF) for p in pieces),
+        in_specs=[vmem] * n_in,
+        out_specs=(vmem,) * 3 + (pl.BlockSpec(memory_space=pl.ANY),) * m,
+        scratch_shapes=scratch,
         compiler_params=pltpu.CompilerParams(
             collective_id=collective_id, has_side_effects=True
         ),
         cost_estimate=pl.CostEstimate(
-            flops=n * S * t * d, bytes_accessed=40 * n * S * t * d, transcendentals=0
+            flops=2 * S * t * d, bytes_accessed=80 * S * t * d, transcendentals=0
         ),
-    )(*arrays)
+    )(out_part, normed_part, standard, *pieces)
 
 
 def half_lanes(first, second, odd):
@@ -668,6 +750,28 @@
         ),
         out_shape=jax.ShapeDtypeStruct((rows, 3 * pairs * LANES), BF),
     )(j[None].astype(jnp.int32), weight, weight)
+
+
+def pick_up(weight, j, F, S):
+    rows, ff = weight.shape
+    w = ff // (F * S)
+    if w % LANES:
+        split = weight.reshape(rows, F, S, w)
+        return lax.dynamic_index_in_dim(split, j, 2, keepdims=False).reshape(rows, F * w)
+
+    def kernel(j_ref, src, out):
+        out[...] = src[...]
+
+    return pl.pallas_call(
+        kernel,
+        grid_spec=pltpu.PrefetchScalarGridSpec(
+            num_scalar_prefetch=1,
+            grid=(F,),
+            in_specs=[pl.BlockSpec((rows, w), lambda i, j_ref: (0, i * S + j_ref[0]))],
+            out_specs=pl.BlockSpec((rows, w), lambda i, j_ref: (0, i)),
+        ),
+        out_shape=jax.ShapeDtypeStruct((rows, F * w), BF),
+    )(j[None].astype(jnp.int32), weight)
 
 
 def unpack_qkv(gathered, rows, S, pairs):
@@ -796,9 +900,7 @@
     normed_own = (standard * gain + shift).astype(BF)
     upstream_own = cotangent[0]
 
-    up_own = lax.dynamic_index_in_dim(
-        fc1_weight.reshape(rows_d, F, S, block_up), j, 2, keepdims=False
-    ).reshape(rows_d, cols_up)
+    up_own = pick_up(fc1_weight, j, F, S)
     down_own = lax.dynamic_slice_in_dim(fc2_weight, j * block_up, block_up, 0)
     if spread and slots == 1:
         qkv_own = pick_qkv(qkv_weight, j, F, S, pairs)
@@ -821,10 +923,10 @@
     pre_act = dot(normed, w_up) + bias_up
     activated = gelu_tanh(pre_act).astype(BF)
     out_term = jnp.sum(upstream.astype(F32), axis=0).reshape(F, rows_d)
-    (piece_down,) = exchange(S, F, 2, grads=((activated, upstream, rider(out_term, D)),))
-    piece_down, qkv_own = lax.optimization_barrier((piece_down, qkv_own))
-    out_mine = piece_down[block_up, :rows_d].astype(F32)
-    all_down = lax.all_gather(piece_down, "seq", axis=0)
+    piece_down, out_mine = exchange(
+        S, F, 2, grads=((activated, upstream, rider(out_term, D)),), split=True
+    )
+    out_mine = out_mine[0, :rows_d].astype(F32)
 
     grad_act = dot_nt(upstream, w_down)
     grad_pre = jax.vjp(gelu_tanh, pre_act)[1](grad_act)[0].astype(BF)
@@ -833,8 +935,9 @@
     shards = (qkv_own,)
     if spread:
         shards += (lax.dynamic_slice_in_dim(dense_weight, j * block_dense, block_dense, 0),)
-    piece_up, w_qkv, *w_dense = exchange(
-        S, F, 3, grads=((normed, grad_pre, rider(up_term, cols_up)),), shards=shards
+    piece_up, w_qkv, *w_dense, all_down = exchange(
+        S, F, 3, grads=((normed, grad_pre, rider(up_term, cols_up)),), shards=shards,
+        tokens=(piece_down,),
     )
     all_up = lax.all_gather(piece_up, "seq", axis=0)
     w_qkv = w_qkv.reshape(D, qkv_width)
@@ -854,12 +957,11 @@
     if spread:
         grads += ((attended, upstream, None),)
     (piece_qkv,) = exchange(S, F, 4, grads=grads, merge=qkv_width)
-    all_qkv = lax.all_gather(piece_qkv, "seq", axis=0)
-
     partial_out = (dot(attended, w_dense) + dot(activated, w_down)).astype(BF)
     partial_normed = (dot_nt(grad_mixed, w_qkv) + dot_nt(grad_pre, w_up)).astype(BF)
-    branches, grad_normed = seq_sum(
-        S, F, 5, (partial_out.reshape(S, tok, D), partial_normed.reshape(S, tok, D))
+    branches, grad_normed, ln_mine, all_qkv = token_sums(
+        S, F, 5, partial_out.reshape(S, tok, D), partial_normed.reshape(S, tok, D),
+        standard, (piece_qkv,),
     )
     result = (inputs + branches + (b_dense + b_down)).astype(BF)
     scaled = grad_normed * gain
@@ -868,9 +970,6 @@
         - jnp.mean(scaled, axis=-1, keepdims=True)
         - standard * jnp.mean(scaled * standard, axis=-1, keepdims=True)
     )
-    ln_terms = jnp.stack([jnp.sum(grad_normed * standard, axis=0), jnp.sum(grad_normed, axis=0)])
-    ln_terms = lax.psum(ln_terms, ("seq", "fsdp"))
-    ln_mine = lax.dynamic_slice_in_dim(ln_terms, f * rows_d, rows_d, 1)
 
     grad_down = unpack_rows(all_down, block_up)
     grad_up = unpack_cols(all_up, rows_d, F)

time: 693 us -> 594 us (0.86); the launches traced: 682 us -> 591 us
  blocking collectives: 94.2 us -> 9.84 us
  local copies, waits for them, and re-layouts: 45.9 us -> 23.2 us
  Pallas kernels: 461 us -> 475 us
    psum x1 -> x0, blocking collectives: 84.4 us -> none  [body(): ln_terms = lax.psum(ln_terms, ('seq', 'fsdp'))]
    pallas_call x1 -> x2, Pallas kernels: 129 us -> 142 us  [the longest x1 139 us: token_sums(): pl.pallas_call(kernel, out_shape=(full, full, jax.ShapeDtypeStruct((LN_RO...]
    unnamed x50 -> x48, local copies, waits for them, and re-layouts: 17.8 us -> 5.46 us
    dynamic_slice x1 -> x0, local copies, waits for them, and re-layouts: 10.9 us -> none  [body(): lax.dynamic_index_in_dim(fc1_weight.reshape(rows_d, F, S, block_up), j, 2...]
  transfers between devices with their start and end apart: 3 -> 1, of which waited for: 0 -> 0; matrix products, arithmetic and copies ran while one was open for 8% -> 9% of each run, Pallas kernels for 33% -> 40%
where the time goes in v3:
time: 594 us; the launch traced here: 591 us
  Pallas kernels  475 us (80%)
  matrix products  50.3 us (8%)
  local copies, waits for them, and re-layouts  23.2 us (4%)
  other arithmetic  18 us (3%)
  between operations  14.6 us (2%)
  blocking collectives  9.84 us (2%)
    pallas_call x4, Pallas kernels, exchange(): pl.pallas_call(kernel, out_shape=tuple(outs), in_specs=in_specs, out_spec...  277 us
    pallas_call x1, Pallas kernels, token_sums(): pl.pallas_call(kernel, out_shape=(full, full, jax.ShapeDtypeStruct((LN_RO...  139 us
    dot_general x4, matrix products, dot_nt(): lax.dot_general(left, right, (((1,), (1,)), ((), ())), preferred_element_...  26.6 us
    dot_general x4, matrix products, dot(): lax.dot_general(left, right, (((1,), (0,)), ((), ())), preferred_element_...  23.7 us
    pallas_call x1, Pallas kernels, attention(): pl.pallas_call(functools.partial(attention_kernel, rows), grid=(pairs,),...  21.5 us
  transfers between devices with their start and end apart: 1, of which 0 were waited for; matrix products, arithmetic and copies ran while one was open for 9% of the time, Pallas kernels for 40%

profile of v3, /device:TPU:0, one launch (start us, length us, event | category | flops | bytes accessed | tf_op | source)
XLA Modules:
  0.0 590.6 jit_solution(17643369677740839310)
XLA Ops:
  12.2 9.8 %all-gather.2 = bf16[4,1,5632]{2,1,0:T(2,128)(2,1)S(1)} all-gather(bf16[1,1,5632]{2,1,0:T(2,128)(2,1)S(1)} %reshape.174), channel_id=2, replica_groups=mesh['seq'=8,'fsdp'=4] {'fsdp'}, dimensions={0}, use_global_device_ids=true | all-gather | bytes 56320 | tf_op jit(solution)/shard_map/all_gather | solution.py:888
  24.7 3.4 shard_map.220.refs_0_
  28.1 4.8 shard_map.222.refs_3_
  32.9 2.3 constant_dynamic-slice_fusion.3.refs_1_
  35.2 1.6 fusion.9
  36.7 74.8 %shard_map.221 = (bf16[4,512,1024]{2,1,0:T(8,128)(2,1)}, bf16[4,256,2048]{2,1,0:T(8,128)(2,1)}, bf16[8,128,2048]{2,1,0:T(8,128)(2,1)}, bf16[8,128,2048]{2,1,0:T(8,128)(2,1)}) custom-call(bf16[512,1024]{1,0:T(8,128)(2,1)} %shard_map.220.refs_0_, bf16[256,2048]{1,0:T(8,128)(2,1)} %constant_dynamic-slice_fusion.3.refs_1_, ...), custom_call_target="tpu_custom_call" | custom-call | bytes 335544320 | tf_op jit(solution)/shard_map/pallas_call | solution.py:513
  111.6 3.0 convert_reduce_fusion
  115.0 8.2 %fusion.18 = f32[1024,1024]{1,0:T(8,128)} fusion(bf16[1024,2048]{1,0:T(8,128)(2,1)} %bitcast.139, bf16[2048,1024]{1,0:T(8,128)(2,1)S(1)} %bitcast.135), kind=kOutput, calls=%fused_computation.60 | convolution fusion | flops 4294967296 | bytes 12582912 | tf_op jit(solution)/shard_map/dot_general | solution.py:22
  123.2 12.2 %convert_reduce_fusion.1 = (f32[1024]{0:T(1024)S(1)}, bf16[1024,1024]{1,0:T(8,128)(2,1)}, bf16[1024,1024]{1,0:T(8,128)(2,1)}) fusion(f32[1024,1024]{1,0:T(8,128)} %fusion.18, f32[1024]{0:T(1024)S(1)} %bitcast.132, bf16[1024,2048]{1,0:T(8,128)(2,1)} %bitcast.100, bf16[1024,2048]{1,0:T(8,128)(2,1)} %bitcast.137), kind=kOutput, calls=%fused_computation.13 | convolution fusion | flops 4321180672 | bytes 16785408 | tf_op jit(solution)/shard_map/dot_general | solution.py:26
  137.7 57.5 %shard_map.223 = (bf16[256,2048]{1,0:T(8,128)(2,1)}, bf16[16,2048]{1,0:T(8,128)(2,1)}) custom-call(bf16[1024,1024]{1,0:T(8,128)(2,1)} %get-tuple-element.50.refs_0_, bf16[1024,2048]{1,0:T(8,128)(2,1)} %bitcast.101, f32[4,16,2048]{2,1,0:T(8,128)} %pad.13.refs_2_), custom_call_target="tpu_custom_call" | custom-call | flops 4294967296 | bytes 22282240 | tf_op jit(solution)/shard_map/pallas_call | solution.py:513
  195.3 88.7 %shard_map.224 = (bf16[528,1024]{1,0:T(8,128)(2,1)}, bf16[4,512,768]{2,1,0:T(8,128)(2,1)}, bf16[4,64,2048]{2,1,0:T(8,128)(2,1)}, bf16[8,256,2048]{2,1,0:T(8,128)(2,1)}) custom-call(bf16[1024,2048]{1,0:T(8,128)(2,1)} %bitcast.140, bf16[1024,1024]{1,0:T(8,128)(2,1)} %get-tuple-element.47.refs_1_, f32[4,16,1024]{2,1,0:T(8,128)} %pad.12.refs_2_, ...), custom_call_target="tpu_custom_call" | custom-call | flops 4294967296 | bytes 273285120 | tf_op jit(solution)/shard_map/pallas_call | solution.py:513
  284.1 1.9 multiply_sine_fusion
  286.1 1.8 concatenate.24.sin_low
  287.9 1.7 concatenate.25.sin_high
  290.9 1.7 concatenate.23.cos
  292.6 4.6 convolution_convert_fusion.grad_out
  297.3 5.1 convolution_add_fusion.proj
  302.3 21.5 %shard_map.225 = (bf16[1024,256]{1,0:T(8,128)(2,1)}, bf16[1024,768]{1,0:T(8,128)(2,1)}) custom-call(f32[1024,768]{1,0:T(8,128)} %convolution_add_fusion.proj, bf16[1024,256]{1,0:T(8,128)(2,1)} %convolution_convert_fusion.grad_out, f32[1024,128]{1,0:T(8,128)} %concatenate.23.cos, f32[1024,128]{1,0:T(8,128)} %concatenate.24.sin_low, ...), custom_call_target="tpu_custom_call" | custom-call | flops 3758096384 | bytes 6291456 | tf_op jit(solution)/shard_map/pallas_call | solution.py:108
  323.8 1.7 convert_reduce_fusion.2
  326.2 55.9 %shard_map.226.refs_3_ = bf16[720,768]{1,0:T(8,128)(2,1)} custom-call(bf16[1024,2048]{1,0:T(8,128)(2,1)} %bitcast.141, bf16[1024,768]{1,0:T(8,128)(2,1)} %get-tuple-element.36.refs_1_, f32[4,16,768]{2,1,0:T(8,128)} %pad.14.refs_2_, bf16[1024,256]{1,0:T(8,128)(2,1)} %get-tuple-element.35.refs_3_, bf16[1024,2048]{1,0:T(8,128)(2,1)} %bitcast.103), custom_call_target="tpu_custom_call" | custom-call | flops 4294967296 | bytes 22118400 | tf_op jit(solution)/shard_map/pallas_call | solution.py:513
  382.1 7.0 %fusion.19 = f32[1024,2048]{1,0:T(8,128)S(1)} fusion(bf16[1024,1024]{1,0:T(8,128)(2,1)} %get-tuple-element.50.refs_0_, bf16[1024,2048]{1,0:T(8,128)(2,1)} %bitcast.138), kind=kOutput, calls=%fused_computation.61 | convolution fusion | flops 4294967296 | bytes 14680064 | tf_op jit(solution)/shard_map/dot_general | solution.py:22
  389.2 3.4 add_convert_fusion.1
  392.6 3.5 fusion.20
  396.1 6.3 %add_convert_fusion = bf16[1024,2048]{1,0:T(8,128)(2,1)} fusion(f32[1024,2048]{1,0:T(8,128)S(1)} %fusion.20, bf16[1024,1024]{1,0:T(8,128)(2,1)S(1)} %copy-done.17, bf16[2048,1024]{1,0:T(8,128)(2,1)S(1)} %bitcast.136), kind=kOutput, calls=%fused_computation | convolution fusion | flops 4299161600 | bytes 18874368 | tf_op jit(solution)/shard_map/dot_general | solution.py:26
  402.4 138.6 %shard_map.227 = (f32[128,2048]{1,0:T(8,128)}, f32[128,2048]{1,0:T(8,128)}, f32[8,512]{1,0:T(8,128)}, bf16[8,720,768]{2,1,0:T(8,128)(2,1)}) custom-call(bf16[8,128,2048]{2,1,0:T(8,128)(2,1)} %bitcast.97, bf16[8,128,2048]{2,1,0:T(8,128)(2,1)} %bitcast.104, f32[128,2048]{1,0:T(8,128)} %get-tuple-element.51.refs_2_, bf16[720,768]{1,0:T(8,128)(2,1)} %shard_map.226.refs_3_), custom_call_target="tpu_custom_call" | custom-call | flops 4194304 | bytes 167772160 | tf_op jit(solution)/shard_map/pallas_call | solution.py:698
  541.0 9.1 %shard_map.228 = f32[512,6144]{1,0:T(8,128)} custom-call(bf16[8,720,768]{2,1,0:T(8,128)(2,1)} %get-tuple-element.40.src), custom_call_target="tpu_custom_call" | custom-call | tf_op jit(solution)/shard_map/pallas_call | solution.py:788
  552.4 10.4 %shard_map.230 = f32[2048,2048]{1,0:T(8,128)} custom-call(bf16[8,256,2048]{2,1,0:T(8,128)(2,1)} %get-tuple-element.43.src), custom_call_target="tpu_custom_call" | custom-call | tf_op jit(solution)/shard_map/pallas_call | solution.py:823
  564.5 1.4 fusion.17
  565.9 1.6 fusion.16
  567.5 2.6 maximum_convert_fusion
  570.0 1.7 add_bitcast_fusion
  571.8 9.9 %shard_map.229 = f32[512,8192]{1,0:T(8,128)} custom-call(bf16[8,528,1024]{2,1,0:T(8,128)(2,1)} %bitcast.98), custom_call_target="tpu_custom_call" | custom-call | tf_op jit(solution)/shard_map/pallas_call | solution.py:808
  (88 shorter events, 18.4 us)
Async XLA Ops:
  7.2 129.8 %copy-start = (bf16[512,2048]{1,0:T(8,128)(2,1)S(1)}, bf16[512,2048]{1,0:T(8,128)(2,1)}, u32[]{:S(2)}) copy-start(bf16[512,2048]{1,0:T(8,128)(2,1)} %param.19) | copy-start | bytes 6291460
  7.2 564.6 %all-gather.5.cloned.1.call-start = ((), (), s32[]{:S(2)}) async-start(), calls=%async_computation | async-start | bytes 9732096 | tf_op jit(solution)/shard_map/all_gather | solution.py:942
  28.1 7.1 %copy-start.2 = (bf16[1,128,2048]{2,1,0:T(8,128)(2,1)S(1)}, bf16[1,128,2048]{2,1,0:T(8,128)(2,1)}, u32[]{:S(2)}) copy-start(bf16[1,128,2048]{2,1,0:T(8,128)(2,1)} %param.14) | copy-start | bytes 1572868
  111.6 3.5 copy-start.12
  195.3 88.8 %copy-start.10 = (s32[1,1024]{1,0:T(1,128)S(1)}, s32[1,1024]{1,0:T(1,128)}, u32[]{:S(2)}) copy-start(s32[1,1024]{1,0:T(1,128)} %seg_row.1) | copy-start | bytes 12292
  289.6 3.0 copy-start.6
  292.6 4.6 copy-start.14
  292.6 4.6 copy-start.15
  382.1 7.1 %copy-start.7 = (bf16[4,64,2048]{2,1,0:T(8,128)(2,1)S(1)}, bf16[4,64,2048]{2,1,0:T(8,128)(2,1)}, u32[]{:S(2)}) copy-start(bf16[4,64,2048]{2,1,0:T(8,128)(2,1)} %get-tuple-element.34) | copy-start | bytes 3145732
  382.1 7.1 %copy-start.9 = (bf16[1024,256]{1,0:T(8,128)(2,1)S(1)}, bf16[1024,256]{1,0:T(8,128)(2,1)}, u32[]{:S(2)}) copy-start(bf16[1024,256]{1,0:T(8,128)(2,1)} %get-tuple-element.35.refs_3_) | copy-start | bytes 1572868
  389.2 3.4 copy-start.5
  389.2 3.4 copy-start.16
  392.6 3.5 copy-start.13
  392.6 3.5 copy-start.17
  552.4 11.7 %copy-start.3 = (f32[128,2048]{1,0:T(8,128)S(1)}, f32[128,2048]{1,0:T(8,128)}, u32[]{:S(2)}) copy-start(f32[128,2048]{1,0:T(8,128)} %get-tuple-element.38) | copy-start | bytes 3145732
  563.5 19.5 %copy-start.11 = (f32[1,512]{1,0:T(1,128)}, f32[1,512]{1,0:T(1,128)S(1)}, u32[]{:S(2)}) copy-start(f32[1,512]{1,0:T(1,128)S(1)} %slice_convert_fusion.3) | copy-start | bytes 6148
  565.8 4.2 copy-start.4
  565.8 4.2 copy-start.8
  571.8 11.8 %copy-start.1 = (bf16[512,2048]{1,0:T(8,128)(2,1)S(1)}, bf16[512,2048]{1,0:T(8,128)(2,1)}, u32[]{:S(2)}) copy-start(bf16[512,2048]{1,0:T(8,128)(2,1)} %param.19) | copy-start | bytes 6291460
Sparse Core Ops, SparseCore 0:
  284.2 83.2 all-gather.4
